TPU v7x, 256 devices: a whole 4x4x8 slice. The times are simulated.
256 devices in a mesh: row: 8 (over y, core), th: 8 (over z), ph: 4 (over x).
Axes of the slice: x: 4, y: 4, z: 8, core: 2. Of those that a mesh axis runs over, the one named last changes fastest.
Arguments:
- fields: float32 [6, 128, 128, 512], P(None, 'row', 'th', 'ph'), may hold values from -6 to 6
- lapse_field: float32 [128, 128, 512], P('row', 'th', 'ph'), may hold values from 0.3 to 1
- excision: int32 [128, 128, 512], P('row', 'th', 'ph'), may hold values 0 or 1
- sample_cells: int32 [128, 128, 4], P('row', 'th', 'ph'), may hold values from 0 to 127
- old_basis: float32 [252, 196608], P(None, ('row', 'th', 'ph'))
Outputs:
- new_fields: float32 [6, 128, 128, 512], P(None, 'row', 'th', 'ph')
- basis_out: float32 [256, 196608], P(None, ('row', 'th', 'ph'))
- factor: float32 [256, 256], replicated
Inputs may be any that keep to these rules, and one draw needn't show every extreme that they name: `excision`: 1 marks an excised cell.
All inputs are finite; a program needn't handle non-finite values. No bound on the sum of `excision` on one device may be relied on, other than what follows from the above.
Results may differ from a plain program's by a relative error of at most 0.007.
Values sent between devices are 32-bit elements; how exact they have to be, the bound alone decides.
A program may use at most 64 MiB of HBM per device.

v0:
```python
import math

import jax
import jax.numpy as jnp
from jax import lax
from jax.sharding import PartitionSpec as P

SPACING = 128


damping_rate = 3.0
time_step = 0.3
azimuth_gain = 5.0


def with_halo(block, sides, width, periodic):
    for axis, dim in sides:
        count = lax.axis_size(axis)
        forward = [(i, i + 1) for i in range(count - 1)]
        if periodic:
            forward.append((count - 1, 0))
        backward = [(target, source) for source, target in forward]
        low = lax.ppermute(
            lax.slice_in_dim(block, block.shape[dim] - width, None, axis=dim), axis, forward
        )
        high = lax.ppermute(lax.slice_in_dim(block, 0, width, axis=dim), axis, backward)
        block = jnp.concatenate([low, block, high], axis=dim)
    return block


def shifted(padded, axis_dim, offset):
    lengths = [padded.shape[0] - 4, padded.shape[1] - 4, padded.shape[2] - 4]
    starts = [2, 2, 2]
    starts[axis_dim] = 2 + offset
    return padded[
        starts[0] : starts[0] + lengths[0],
        starts[1] : starts[1] + lengths[1],
        starts[2] : starts[2] + lengths[2],
    ]


def derivative(padded, axis_dim):
    near_diff = shifted(padded, axis_dim, 1) - shifted(padded, axis_dim, -1)
    far_diff = shifted(padded, axis_dim, 2) - shifted(padded, axis_dim, -2)
    spacing_gain = azimuth_gain if axis_dim == 2 else 1.0
    return (8.0 * near_diff - far_diff) * (spacing_gain / 12.0)


def curl_of(padded, start_comp):
    first_part = padded[start_comp]
    second_part = padded[start_comp + 1]
    third_part = padded[start_comp + 2]
    return jnp.stack(
        [
            derivative(third_part, 1) - derivative(second_part, 2),
            derivative(first_part, 2) - derivative(third_part, 0),
            derivative(second_part, 0) - derivative(first_part, 1),
        ]
    )


def rates(padded, fields, damping):
    electric = curl_of(padded, 3) - damping_rate * damping * fields[:3]
    magnetic = -curl_of(padded, 0) - damping_rate * damping * fields[3:]
    return jnp.concatenate([electric, magnetic])


def padded_each(product):
    beside_all = with_halo(product, (("ph", 3),), 2, True)
    return with_halo(beside_all, (("row", 1), ("th", 2)), 2, False)


def on_device(fields, lapse_field, excision, sample_cells, old_basis):
    damping = excision.astype(jnp.float32)
    rad_cells = fields.shape[1]
    pol_cells = fields.shape[2]
    azi_cells = fields.shape[3]
    rad_total = rad_cells * lax.axis_size("row")
    pol_total = pol_cells * lax.axis_size("th")
    section_one = fields + time_step * rates(padded_each(lapse_field * fields), fields, damping)
    rate_two = rates(padded_each(lapse_field * section_one), section_one, damping)
    new_fields = 0.5 * (fields + section_one + time_step * rate_two)
    rad_index = (lax.axis_index("row") * rad_cells + jnp.arange(rad_cells)).astype(jnp.float32)
    pol_index = (lax.axis_index("th") * pol_cells + jnp.arange(pol_cells)).astype(jnp.float32)
    radius = 1.0 + 2.0 * (rad_index + 0.5) / rad_total
    polar = jnp.pi * (pol_index + 0.5) / pol_total
    weight = radius[:, None] * jnp.sqrt(jnp.sin(polar))[None, :]
    groups = azi_cells // SPACING
    chosen = jnp.arange(SPACING)[None, None, None, :] == sample_cells[:, :, :, None]
    weighted = jnp.where(chosen, weight[:, :, None, None], 0.0)

    def sample(field_set):
        grouped = field_set.reshape(6, rad_cells, pol_cells, groups, SPACING)
        return jnp.sum(grouped * weighted[None], axis=-1)

    snap_one = sample(section_one)
    snap_two = sample(new_fields)
    snapshot = jnp.stack(
        [
            snap_one[:3].reshape(-1),
            snap_one[3:].reshape(-1),
            snap_two[:3].reshape(-1),
            snap_two[3:].reshape(-1),
        ]
    )
    matrix = jnp.concatenate([old_basis, snapshot], axis=0)
    gram_sum = lax.psum(
        jnp.dot(matrix, matrix.T, precision=lax.Precision.HIGHEST), ("row", "th", "ph")
    )
    factor_low = lax.linalg.cholesky(gram_sum)
    solved = lax.linalg.triangular_solve(factor_low, matrix, left_side=True, lower=True)
    row_scale = math.sqrt(
        old_basis.shape[1] * lax.axis_size("row") * lax.axis_size("th") * lax.axis_size("ph")
    )
    return (new_fields, solved * row_scale, factor_low.T / row_scale)


def solution(mesh):
    return jax.shard_map(
        on_device,
        mesh=mesh,
        in_specs=(
            P(None, "row", "th", "ph"),
            P("row", "th", "ph"),
            P("row", "th", "ph"),
            P("row", "th", "ph"),
            P(None, ("row", "th", "ph")),
        ),
        out_specs=(P(None, "row", "th", "ph"), P(None, ("row", "th", "ph")), P()),
        check_vma=False,
    )
```

profile of v0, /device:TPU:1, one launch (start us, length us, event | category | flops | bytes accessed | tf_op | source)
XLA Modules:
  0.0 411.3 jit_solution(14045041573448911381)
XLA Ops:
  9.3 2.1 collective-permute-start
  16.4 5.2 %collective-permute-start.2 = (f32[6,2,16,132]{3,2,1,0:T(8,128)S(1)}, f32[6,2,16,132]{3,2,1,0:T(8,128)S(1)}, u32[]{:S(2)}, u32[]{:S(2)}) collective-permute-start(f32[6,2,16,132]{3,2,1,0:T(8,128)S(1)} %get-tuple-element.56), channel_id=1, source_target_pairs={{0,32},{32,64},{64,96},{96,128},{128,160},{160,192},{192,224},{1,3... | collective-permute-start | bytes 304136 | tf_op jit(solution)/shard_map/ppermute | solution.py:23
  21.6 1.9 collective-permute-start.3
  24.2 4.4 %collective-permute-done.3 = f32[6,2,16,132]{3,2,1,0:T(8,128)S(1)} collective-permute-done((f32[6,2,16,132]{3,2,1,0:T(8,128)S(1)}, f32[6,2,16,132]{3,2,1,0:T(8,128)S(1)}, u32[]{:S(2)}, u32[]{:S(2)}) %collective-permute-start.3) | collective-permute-done | bytes 101408 | tf_op jit(solution)/shard_map/ppermute | solution.py:26
  29.3 3.6 collective-permute-start.4
  34.2 1.8 collective-permute-done.4
  36.0 4.0 collective-permute-done.5
  47.2 1.5 collective-permute-start.7
  51.6 6.7 %collective-permute-start.8 = (f32[6,2,16,132]{3,2,1,0:T(8,128)S(1)}, f32[6,2,16,132]{3,2,1,0:T(8,128)S(1)}, u32[]{:S(2)}, u32[]{:S(2)}) collective-permute-start(f32[6,2,16,132]{3,2,1,0:T(8,128)S(1)} %get-tuple-element.54), channel_id=1, source_target_pairs={{0,32},{32,64},{64,96},{96,128},{128,160},{160,192},{192,224},{1,3... | collective-permute-start | bytes 304136 | tf_op jit(solution)/shard_map/ppermute | solution.py:23
  58.3 1.9 collective-permute-start.9
  60.9 4.4 %collective-permute-done.9 = f32[6,2,16,132]{3,2,1,0:T(8,128)S(1)} collective-permute-done((f32[6,2,16,132]{3,2,1,0:T(8,128)S(1)}, f32[6,2,16,132]{3,2,1,0:T(8,128)S(1)}, u32[]{:S(2)}, u32[]{:S(2)}) %collective-permute-start.9) | collective-permute-done | bytes 101408 | tf_op jit(solution)/shard_map/ppermute | solution.py:26
  66.0 3.5 collective-permute-start.10
  69.5 1.5 collective-permute-start.11
  71.2 1.5 collective-permute-done.10
  72.7 5.1 %collective-permute-done.11 = f32[6,20,2,132]{3,2,1,0:T(2,128)S(1)} collective-permute-done((f32[6,20,2,132]{3,2,1,0:T(2,128)S(1)}, f32[6,20,2,132]{3,2,1,0:T(2,128)S(1)}, u32[]{:S(2)}, u32[]{:S(2)}) %collective-permute-start.11) | collective-permute-done | bytes 126752 | tf_op jit(solution)/shard_map/ppermute | solution.py:26
  82.7 1.5 fusion.117
  84.2 254.2 %all-reduce.3.cloned.1.call-done = f32[256,256]{0,1:T(8,128)} async-done(((f32[256,256]{0,1:T(8,128)}), f32[256,256]{0,1:T(8,128)}) %all-reduce.3.cloned.1.call-update) | async-done | bytes 262160 | tf_op jit(solution)/shard_map/psum | solution.py:107
  340.6 11.7 %cholesky.50 = f32[128,128]{1,0:T(8,128)S(1)} custom-call(f32[128,128]{1,0:T(8,128)S(1)} %cholesky.118), custom_call_target="Cholesky" | custom-call | tf_op jit(solution)/shard_map/cholesky | solution.py:110
  352.3 9.8 %custom-call.11 = f32[1,128,128]{1,2,0:T(8,128)S(1)} custom-call(f32[1,128,128]{2,1,0:T(8,128)S(1)} %get-tuple-element.79), custom_call_target="InvertDiagBlocksLowerTriangular" | custom-call | tf_op jit(solution)/shard_map/cholesky | solution.py:110
  362.6 11.7 %cholesky.105 = f32[128,128]{1,0:T(8,128)S(1)} custom-call(f32[128,128]{1,0:T(8,128)S(1)} %convolution_subtract_fusion.1), custom_call_target="Cholesky" | custom-call | tf_op jit(solution)/shard_map/cholesky | solution.py:110
  377.2 4.0 while.1
  377.8 1.4 bitcast_dynamic-update-slice_fusion.2
  379.8 1.4 bitcast_dynamic-update-slice_fusion.2
  381.2 19.9 %custom-call.12 = f32[2,128,128]{1,2,0:T(8,128)S(1)} custom-call(f32[2,128,128]{2,1,0:T(8,128)S(1)} %get-tuple-element.10), custom_call_target="InvertDiagBlocksLowerTriangular" | custom-call | tf_op jit(solution)/shard_map/triangular_solve | solution.py:111
  (87 shorter events, 34.7 us)
Async XLA Ops:
  7.2 331.3 %all-reduce.3.cloned.1.call-start = ((), (), s32[]{:S(2)}) async-start(), calls=%async_computation | async-start | bytes 524288 | tf_op jit(solution)/shard_map/psum | solution.py:107
  9.3 5.4 %collective-permute-start = (f32[6,16,16,2]{2,1,3,0:T(8,128)S(1)}, f32[6,16,16,2]{2,1,3,0:T(8,128)S(1)}, u32[]{:S(2)}, u32[]{:S(2)}) collective-permute-start(f32[6,16,16,2]{2,1,3,0:T(8,128)S(1)} %copy.55), channel_id=1, source_target_pairs={{0,1},{1,2},{2,3},{3,0},{4,5},{5,6},{6,7},{7,4},{8,9},{9,10},{10,1... | collective-permute-start | bytes 36872 | tf_op jit(solution)/shard_map/ppermute | solution.py:23
  12.0 3.5 collective-permute-start.1
  16.2 18.0 %copy-start.4 = (s32[16,16,128]{2,1,0:T(8,128)S(1)}, s32[16,16,128]{2,1,0:T(8,128)}, u32[]{:S(2)}) copy-start(s32[16,16,128]{2,1,0:T(8,128)} %param.7) | copy-start | bytes 393220
  16.4 7.8 %collective-permute-start.2 = (f32[6,2,16,132]{3,2,1,0:T(8,128)S(1)}, f32[6,2,16,132]{3,2,1,0:T(8,128)S(1)}, u32[]{:S(2)}, u32[]{:S(2)}) collective-permute-start(f32[6,2,16,132]{3,2,1,0:T(8,128)S(1)} %get-tuple-element.56), channel_id=1, source_target_pairs={{0,32},{32,64},{64,96},{96,128},{128,160},{160,192},{192,224},{1,3... | collective-permute-start | bytes 304136 | tf_op jit(solution)/shard_map/ppermute | solution.py:23
  21.6 7.0 %collective-permute-start.3 = (f32[6,2,16,132]{3,2,1,0:T(8,128)S(1)}, f32[6,2,16,132]{3,2,1,0:T(8,128)S(1)}, u32[]{:S(2)}, u32[]{:S(2)}) collective-permute-start(f32[6,2,16,132]{3,2,1,0:T(8,128)S(1)} %get-tuple-element.57), channel_id=1, source_target_pairs={{32,0},{64,32},{96,64},{128,96},{160,128},{192,160},{224,192},{33,... | collective-permute-start | bytes 304136 | tf_op jit(solution)/shard_map/ppermute | solution.py:26
  29.3 6.7 %collective-permute-start.4 = (f32[6,20,2,132]{3,2,1,0:T(2,128)S(1)}, f32[6,20,2,132]{3,2,1,0:T(2,128)S(1)}, u32[]{:S(2)}, u32[]{:S(2)}) collective-permute-start(f32[6,20,2,132]{3,2,1,0:T(2,128)S(1)} %get-tuple-element.51), channel_id=1, source_target_pairs={{0,4},{4,8},{8,12},{12,16},{16,20},{20,24},{24,28},{1,5},{5,9},{9,... | collective-permute-start | bytes 380168 | tf_op jit(solution)/shard_map/ppermute | solution.py:23
  32.9 7.1 %collective-permute-start.5 = (f32[6,20,2,132]{3,2,1,0:T(2,128)S(1)}, f32[6,20,2,132]{3,2,1,0:T(2,128)S(1)}, u32[]{:S(2)}, u32[]{:S(2)}) collective-permute-start(f32[6,20,2,132]{3,2,1,0:T(2,128)S(1)} %get-tuple-element.52), channel_id=1, source_target_pairs={{4,0},{8,4},{12,8},{16,12},{20,16},{24,20},{28,24},{5,1},{9,5},{13... | collective-permute-start | bytes 380168 | tf_op jit(solution)/shard_map/ppermute | solution.py:26
  41.8 1.2 copy-start
  42.4 1.0 copy-start.3
  45.3 4.7 %collective-permute-start.6 = (f32[6,16,16,2]{2,1,3,0:T(8,128)S(1)}, f32[6,16,16,2]{2,1,3,0:T(8,128)S(1)}, u32[]{:S(2)}, u32[]{:S(2)}) collective-permute-start(f32[6,16,16,2]{2,1,3,0:T(8,128)S(1)} %copy.59), channel_id=1, source_target_pairs={{0,1},{1,2},{2,3},{3,0},{4,5},{5,6},{6,7},{7,4},{8,9},{9,10},{10,1... | collective-permute-start | bytes 36872 | tf_op jit(solution)/shard_map/ppermute | solution.py:23
  47.2 3.5 collective-permute-start.7
  51.4 19.6 %copy-start.5 = (s32[16,16,1]{1,2,0:T(1,128)S(1)}, s32[16,16,1]{1,2,0:T(1,128)}, u32[]{:S(2)}) copy-start(s32[16,16,1]{1,2,0:T(1,128)} %param.8) | copy-start | bytes 3076
  51.6 9.3 %collective-permute-start.8 = (f32[6,2,16,132]{3,2,1,0:T(8,128)S(1)}, f32[6,2,16,132]{3,2,1,0:T(8,128)S(1)}, u32[]{:S(2)}, u32[]{:S(2)}) collective-permute-start(f32[6,2,16,132]{3,2,1,0:T(8,128)S(1)} %get-tuple-element.54), channel_id=1, source_target_pairs={{0,32},{32,64},{64,96},{96,128},{128,160},{160,192},{192,224},{1,3... | collective-permute-start | bytes 304136 | tf_op jit(solution)/shard_map/ppermute | solution.py:23
  58.3 7.0 %collective-permute-start.9 = (f32[6,2,16,132]{3,2,1,0:T(8,128)S(1)}, f32[6,2,16,132]{3,2,1,0:T(8,128)S(1)}, u32[]{:S(2)}, u32[]{:S(2)}) collective-permute-start(f32[6,2,16,132]{3,2,1,0:T(8,128)S(1)} %get-tuple-element.55), channel_id=1, source_target_pairs={{32,0},{64,32},{96,64},{128,96},{160,128},{192,160},{224,192},{33,... | collective-permute-start | bytes 304136 | tf_op jit(solution)/shard_map/ppermute | solution.py:26
  66.0 6.7 %collective-permute-start.10 = (f32[6,20,2,132]{3,2,1,0:T(2,128)S(1)}, f32[6,20,2,132]{3,2,1,0:T(2,128)S(1)}, u32[]{:S(2)}, u32[]{:S(2)}) collective-permute-start(f32[6,20,2,132]{3,2,1,0:T(2,128)S(1)} %get-tuple-element.49), channel_id=1, source_target_pairs={{0,4},{4,8},{8,12},{12,16},{16,20},{20,24},{24,28},{1,5},{5,9},{9,... | collective-permute-start | bytes 380168 | tf_op jit(solution)/shard_map/ppermute | solution.py:23
  69.5 8.2 %collective-permute-start.11 = (f32[6,20,2,132]{3,2,1,0:T(2,128)S(1)}, f32[6,20,2,132]{3,2,1,0:T(2,128)S(1)}, u32[]{:S(2)}, u32[]{:S(2)}) collective-permute-start(f32[6,20,2,132]{3,2,1,0:T(2,128)S(1)} %get-tuple-element.50), channel_id=1, source_target_pairs={{4,0},{8,4},{12,8},{16,12},{20,16},{24,20},{28,24},{5,1},{9,5},{13... | collective-permute-start | bytes 380168 | tf_op jit(solution)/shard_map/ppermute | solution.py:26
  79.4 1.5 copy-start.1
  80.9 1.6 copy-start.2
Sparse Core Ops, SparseCore 0:
  84.3 254.0 all-reduce.2
where the time goes:
time: 413 us; the launch traced here: 411 us
  waiting for transfers between devices  280 us (68%)
  other arithmetic  67.8 us (16%)
  starting transfers between devices  31.9 us (8%)
  between operations  15.7 us (4%)
  local copies, waits for them, and re-layouts  12.8 us (3%)
    psum x1, waiting for transfers between devices, on_device(): lax.psum(jnp.dot(matrix, matrix.T, precision=lax.Precision.HIGHEST), ('ro...  254 us
    another operation x7, other arithmetic, on_device(): factor_low = lax.linalg.cholesky(gram_sum)  34.6 us
    ppermute x6, starting transfers between devices, with_halo(): lax.ppermute(lax.slice_in_dim(block, block.shape[dim] - width, None, axis...  22.4 us
    another operation x2, other arithmetic, on_device(): lax.linalg.triangular_solve(factor_low, matrix, left_side=True, lower=True)  19.9 us
    ppermute x6, waiting for transfers between devices, with_halo(): lax.ppermute(lax.slice_in_dim(block, 0, width, axis=dim), axis, backward)  18.2 us
    ppermute x6, starting transfers between devices, with_halo(): lax.ppermute(lax.slice_in_dim(block, 0, width, axis=dim), axis, backward)  9.49 us
  transfers between devices with their start and end apart: 13, of which 12 were waited for; matrix products, arithmetic and copies ran while one was open for 1% of the time, Pallas kernels for 0%

commit v1 on v0

v1 whole, which is shorter than its diff:
```python
import functools
import math

import jax
import jax.numpy as jnp
from jax import lax
from jax.experimental import pallas as pl
from jax.experimental.pallas import tpu as pltpu
from jax.sharding import PartitionSpec as P

MESH = pl.DeviceIdType.MESH
HIGH = lax.Precision.HIGHEST
VMEM = pl.BlockSpec(memory_space=pltpu.VMEM)
ANY = pl.BlockSpec(memory_space=pl.ANY)

damping_rate = 3.0
time_step = 0.3
azimuth_gain = 5.0

SLOT = {0: 0, 3: 1, 2: 2, 5: 3, 1: 4, 4: 5}
EDGE = {0: 0, 3: 1, 1: 2, 4: 3}


def nt(a, b):
    return lax.dot_general(a, b, (((1,), (1,)), ((), ())), precision=HIGH, preferred_element_type=jnp.float32)


def nn(a, b):
    return lax.dot_general(a, b, (((1,), (0,)), ((), ())), precision=HIGH, preferred_element_type=jnp.float32)


def tn(a, b):
    return lax.dot_general(a, b, (((0,), (0,)), ((), ())), precision=HIGH, preferred_element_type=jnp.float32)


def diff(near_high, near_low, far_high, far_low, gain):
    return (8.0 * (near_high - near_low) - (far_high - far_low)) * (gain / 12.0)


def comm_kernel(
    sizes,
    fields_ref, lapse_ref, excision_ref, cells_ref, old_ref,
    new_ref, gram_ref, cross_ref, snap_ref,
    field, lapse, excision, cells, old, mat, section, fresh, weighted, masked,
    padded, polar_out, polar_in, edge_out, edge_in,
    gram, full, pair, plane, deep, cross_plane, cross_deep,
    load_sem, store_sem, halo_send, halo_recv, send_sem, recv_sem,
):
    n_row, n_th, n_ph = sizes
    n_y = n_row // 2
    row, th, ph = lax.axis_index("row"), lax.axis_index("th"), lax.axis_index("ph")
    core, y = lax.rem(row, 2), lax.div(row, 2)
    spot = y * n_ph + ph
    half = n_y * n_ph
    chunks = 2 * half
    owner = core * half + spot
    cr, ct, cp = 16, 16, 128

    loads = [
        pltpu.make_async_copy(source, target, load_sem.at[k])
        for k, (source, target) in enumerate(
            ((old_ref, old), (fields_ref, field), (lapse_ref, lapse), (excision_ref, excision), (cells_ref, cells))
        )
    ]
    for load in loads:
        load.start()

    def place(index):
        which, rest = lax.div(index, half), lax.rem(index, half)
        return {"row": lax.div(rest, n_ph) * 2 + which, "ph": lax.rem(rest, n_ph)}

    def in_plane(d):
        return place(lax.rem(owner + d, chunks))

    def in_half(d):
        return place(core * half + lax.rem(spot + d, half))

    def along(d):
        return {"th": lax.rem(th + d, n_th)}

    barrier = pltpu.get_barrier_semaphore()
    for d in range(1, chunks):
        pl.semaphore_signal(barrier, inc=1, device_id=in_plane(d), device_id_type=MESH)
    for d in range(1, n_th):
        pl.semaphore_signal(barrier, inc=1, device_id=along(d), device_id_type=MESH)

    def send(source, target, device, k):
        copy = pltpu.make_async_remote_copy(
            src_ref=source, dst_ref=target, send_sem=send_sem.at[k], recv_sem=recv_sem.at[k],
            device_id=device, device_id_type=MESH,
        )
        copy.start()

    def landed(ref, k):
        pltpu.make_async_copy(ref, ref, recv_sem.at[k]).wait()

    def left(ref, k):
        pltpu.make_async_copy(ref, ref, send_sem.at[k]).wait()

    lane = lax.broadcasted_iota(jnp.int32, (ct, cp), 1)
    lane_pair = lax.shift_right_logical(lane, 1)

    loads[0].wait()
    mat[0:248] = old[0:248]
    mat[248:252] = old[248:252]
    mat[252:256] = jnp.zeros((4, mat.shape[1]), jnp.float32)
    product = nt(mat[...], mat[...])
    gram[...] = product.reshape(gram.shape)

    def keep_product(stage, c, i, value, edges):
        slot = SLOT[c]
        padded[stage, slot, i + 2, 8:24, :] = value
        if slot < 4:
            for s in range(2):
                polar_out[stage, 0, slot, s, pl.ds(i, 1), :] = value[s : s + 1]
                polar_out[stage, 1, slot, s, pl.ds(i, 1), :] = value[14 + s : 15 + s]
        if c in EDGE:
            t = EDGE[c] * cr + i
            here = lane_pair == t
            edges = (
                jnp.where(here, pltpu.roll(value, 2 * t, 1), edges[0]),
                jnp.where(here, pltpu.roll(value, lax.rem(2 * t + 2, cp), 1), edges[1]),
            )
        return edges

    def no_edges():
        return jnp.zeros((ct, cp), jnp.float32), jnp.zeros((ct, cp), jnp.float32)

    def first_products(i, edges):
        scale = lapse[i]
        for c in range(6):
            edges = keep_product(0, c, i, scale * field[c, i], edges)
        return edges

    def halo_copies(stage):
        rows = ((padded.at[stage, 2:6, 2:4, 8:24, :], padded.at[stage, 2:6, 18:20, 8:24, :], {"row": lax.rem(row + n_row - 1, n_row)}),
                (padded.at[stage, 2:6, 16:18, 8:24, :], padded.at[stage, 2:6, 0:2, 8:24, :], {"row": lax.rem(row + 1, n_row)}))
        polars = ((polar_out.at[stage, 0], polar_in.at[stage, 1], {"th": lax.rem(th + n_th - 1, n_th)}),
                  (polar_out.at[stage, 1], polar_in.at[stage, 0], {"th": lax.rem(th + 1, n_th)}))
        edges = ((edge_out.at[stage, 0], edge_in.at[stage, 1], {"ph": lax.rem(ph + n_ph - 1, n_ph)}),
                 (edge_out.at[stage, 1], edge_in.at[stage, 0], {"ph": lax.rem(ph + 1, n_ph)}))
        return [
            pltpu.make_async_remote_copy(
                src_ref=source, dst_ref=target, send_sem=halo_send.at[stage, k], recv_sem=halo_recv.at[stage, k],
                device_id=device, device_id_type=MESH,
            )
            for k, (source, target, device) in enumerate(rows + polars + edges)
        ]

    def keep_edges(stage, edges):
        edge_out[stage, 0] = edges[0]
        edge_out[stage, 1] = edges[1]

    for load in loads[1:]:
        load.wait()
    keep_edges(0, lax.fori_loop(0, cr, first_products, no_edges()))

    pl.semaphore_wait(barrier, chunks - 1 + n_th - 1)

    halos = [halo_copies(0), halo_copies(1)]
    for copy in halos[0]:
        copy.start()
    other = 1 - core
    send(gram.at[pl.ds(other * half, half)], pair, {"row": y * 2 + other}, 0)

    pol_index = (th * ct + lax.broadcasted_iota(jnp.int32, (ct, cp), 0)).astype(jnp.float32)
    polar = jnp.pi * (pol_index + 0.5) / (n_th * ct)
    polar_weight = jnp.sqrt(jnp.sin(polar))
    chosen = cells[...].T
    for i in range(cr):
        radius = 1.0 + 2.0 * ((row * cr + i).astype(jnp.float32) + 0.5) / (n_row * cr)
        weighted[i] = jnp.where(lane == chosen[:, i : i + 1], polar_weight * radius, 0.0)

    def rates(stage, i, c_values):
        damped = damping_rate * excision[i].astype(jnp.float32)
        lo_edge, hi_edge = edge_in[stage, 0], edge_in[stage, 1]
        for slot in range(4):
            for s in range(2):
                low = polar_in[stage, 0, slot, s, pl.ds(i, 1), :]
                high = polar_in[stage, 1, slot, s, pl.ds(i, 1), :]
                padded[stage, slot, i + 2, 6 + s : 7 + s, :] = jnp.where(th > 0, low, 0.0)
                padded[stage, slot, i + 2, 24 + s : 25 + s, :] = jnp.where(th < n_th - 1, high, 0.0)

        def rad(c):
            get = lambda o: padded[stage, SLOT[c], i + 2 + o, 8:24, :]
            return diff(get(1), get(-1), get(2), get(-2), 1.0)

        def pol(c):
            get = lambda o: padded[stage, SLOT[c], i + 2, 8 + o : 24 + o, :]
            return diff(get(1), get(-1), get(2), get(-2), 1.0)

        def azi(c):
            here = padded[stage, SLOT[c], i + 2, 8:24, :]
            t = EDGE[c] * cr + i
            low = pltpu.roll(lo_edge, cp - 2 - 2 * t, 1)
            high = pltpu.roll(hi_edge, lax.rem(cp - 2 * t, cp), 1)
            far_low = pltpu.roll(jnp.where(lane >= cp - 2, low, here), 2, 1)
            near_low = pltpu.roll(jnp.where(lane >= cp - 1, low, here), 1, 1)
            near_high = pltpu.roll(jnp.where(lane < 1, high, here), cp - 1, 1)
            far_high = pltpu.roll(jnp.where(lane < 2, high, here), cp - 2, 1)
            return diff(near_high, near_low, far_high, far_low, azimuth_gain)

        out = []
        for start, sign in ((3, 1.0), (0, -1.0)):
            curls = (pol(start + 2) - azi(start + 1), azi(start) - rad(start + 2), rad(start + 1) - pol(start))
            for k in range(3):
                c = len(out)
                out.append((curls[k] if sign > 0 else -curls[k]) - damped * c_values[c])
        return out

    def zero_ends(stage):
        low = padded[stage, 2:6, 0:2, 8:24, :]
        padded[stage, 2:6, 0:2, 8:24, :] = jnp.where(row > 0, low, 0.0)
        high = padded[stage, 2:6, 18:20, 8:24, :]
        padded[stage, 2:6, 18:20, 8:24, :] = jnp.where(row < n_row - 1, high, 0.0)

    def first_step(i, edges):
        values = [field[c, i] for c in range(6)]
        rate = rates(0, i, values)
        scale, pick = lapse[i], weighted[i]
        for c in range(6):
            value = values[c] + time_step * rate[c]
            section[c, i] = value
            masked[0, c, pl.ds(pl.multiple_of(i * ct, ct), ct), :] = value * pick
            edges = keep_product(1, c, i, scale * value, edges)
        return edges

    def second_step(i, nothing):
        values = [section[c, i] for c in range(6)]
        rate = rates(1, i, values)
        pick = weighted[i]
        for c in range(6):
            value = 0.5 * (field[c, i] + values[c] + time_step * rate[c])
            fresh[c, i] = value
            masked[1, c, pl.ds(pl.multiple_of(i * ct, ct), ct), :] = value * pick
        return nothing

    landed(pair, 0)
    mine = pl.ds(core * half, half)
    gram[mine] = gram[mine] + pair[...]
    for d in range(1, half):
        send(gram.at[core * half + lax.rem(spot + d, half)], plane.at[d - 1], in_half(d), 1)

    for copy in halos[0]:
        copy.wait_recv()
    zero_ends(0)
    keep_edges(1, lax.fori_loop(0, cr, first_step, no_edges()))
    for copy in halos[1]:
        copy.start()
    ones = jnp.ones((8, cp), jnp.float32)
    sampled_one = nt(ones, masked[0].reshape(6 * cr * ct, cp))

    landed(plane, 1)
    total = gram[owner]
    for d in range(1, half):
        total = total + plane[d - 1]
    deep[0] = total
    for d in range(1, n_th):
        send(deep.at[0], deep.at[d], along(d), 2)

    for copy in halos[1]:
        copy.wait_recv()
    zero_ends(1)
    lax.fori_loop(0, cr, second_step, 0)
    store = pltpu.make_async_copy(fresh, new_ref, store_sem)
    store.start()
    sampled_two = nt(ones, masked[1].reshape(6 * cr * ct, cp))
    width = 3 * cr * ct
    place_row = lax.broadcasted_iota(jnp.int32, (8, width), 0)
    snap = jnp.where(place_row == 4, sampled_one[:, :width], 0.0)
    snap = jnp.where(place_row == 5, sampled_one[:, width:], snap)
    snap = jnp.where(place_row == 6, sampled_two[:, :width], snap)
    snap = jnp.where(place_row == 7, sampled_two[:, width:], snap)
    snap_ref[...] = snap
    mat[248:256] = mat[248:256] + snap
    cross_plane[0] = nt(snap, mat[...])
    for d in range(1, chunks):
        send(cross_plane.at[0], cross_plane.at[d], in_plane(d), 3)

    landed(deep.at[1:], 2)
    total = deep[th]
    for a in range(1, n_th):
        total = total + deep[lax.rem(th - a + n_th, n_th)]
    full[owner] = total
    for d in range(1, half):
        send(full.at[owner], full.at[owner], in_half(d), 4)

    landed(cross_plane.at[1:], 3)
    total = cross_plane[owner]
    for a in range(1, chunks):
        total = total + cross_plane[lax.rem(owner - a + chunks, chunks)]
    cross_deep[0] = total
    for d in range(1, n_th):
        send(cross_deep.at[0], cross_deep.at[d], along(d), 5)

    landed(plane, 4)
    send(full.at[mine], full.at[mine], {"row": y * 2 + other}, 6)

    landed(cross_deep.at[1:], 5)
    total = cross_deep[th]
    for a in range(1, n_th):
        total = total + cross_deep[lax.rem(th - a + n_th, n_th)]
    cross_ref[...] = total

    landed(pair, 6)
    gram_ref[...] = full[...].reshape(gram_ref.shape)

    for stage in range(2):
        for copy in halos[stage]:
            copy.wait_send()
    left(pair, 0)
    left(plane, 1)
    left(deep.at[1:], 2)
    left(cross_plane.at[1:], 3)
    left(plane, 4)
    left(cross_deep.at[1:], 5)
    left(pair, 6)
    store.wait()


def sublane(x, k):
    return jnp.broadcast_to(x[k : k + 1], x.shape)


def eliminate(columns, x, follower=None):
    sub = lax.broadcasted_iota(jnp.int32, x.shape, 0)
    columns = list(columns)
    lows, recips, rows = [], [], []
    solved = jnp.zeros_like(x)
    for k in range(8):
        recip = lax.rsqrt(sublane(columns[k], k))
        low = columns[k] * recip
        for b in range(k + 1, 8):
            columns[b] = columns[b] - low * sublane(low, b)
        wide = jnp.tile(recip, (1, x.shape[1] // 128))
        line = sublane(x, k) * wide
        x = x - jnp.tile(low, (1, x.shape[1] // 128)) * line
        solved = jnp.where(sub == k, line, solved)
        lows.append(low)
        recips.append(recip)
        rows.append(line)
        if follower is not None:
            follower(k, recip, low, line)
    return lows, recips, rows, solved


def spread(tile, first):
    return [jnp.broadcast_to(tile[:, first + b : first + b + 1], (8, 128)) for b in range(8)]


def twice(x):
    return jnp.concatenate([x, x], axis=1)


def leaf(work, upper, inverse):
    for p in range(16):
        r0 = 8 * p
        x = work[r0 : r0 + 8]
        state = {}
        if p < 15:
            state["x"] = work[r0 + 8 : r0 + 16]
            state["e"] = spread(state["x"], r0)

        def follower(k, recip, low, line):
            mine = state["e"][k] * recip
            state["x"] = state["x"] - twice(mine) * line
            for b in range(k + 1, 8):
                state["e"][b] = state["e"][b] - mine * sublane(low, b)

        lows, recips, rows, solved = eliminate(spread(x, r0), x, follower if p < 15 else None)
        lane = lax.broadcasted_iota(jnp.int32, (8, 128), 1)
        sub = lax.broadcasted_iota(jnp.int32, (8, 128), 0)
        upper[r0 : r0 + 8] = jnp.where(lane >= sub + r0, solved[:, :128], 0.0)
        inverse[r0 : r0 + 8] = solved[:, 128:]
        if p < 15:
            work[r0 + 8 : r0 + 16] = state["x"]
        if p < 14:
            back = [None] * 8
            for q in range(7, -1, -1):
                value = rows[q]
                for a in range(q + 1, 8):
                    value = value - twice(sublane(lows[q], a)) * back[a]
                back[q] = value * twice(recips[q])
            for t in range(p + 2, 16):
                tile = work[8 * t : 8 * t + 8]
                for k, column in enumerate(spread(tile, r0)):
                    tile = tile - twice(column) * back[k]
                work[8 * t : 8 * t + 8] = tile


def solve_kernel(
    scale,
    gram_ref, cross_ref, snap_ref, old_ref, new_ref,
    out_new_ref, basis_ref, factor_ref,
    new, old, mat, work, upper, inverse, basis, padded,
    load_sem, store_sem,
):
    loads = [pltpu.make_async_copy(old_ref, old, load_sem.at[0]), pltpu.make_async_copy(new_ref, new, load_sem.at[1])]
    for load in loads:
        load.start()
    row = lax.broadcasted_iota(jnp.int32, (128, 128), 0)
    lane = lax.broadcasted_iota(jnp.int32, (128, 128), 1)
    unit = (row == lane).astype(jnp.float32)
    work[:, :128] = gram_ref[0:128, 0:128]
    work[:, 128:] = unit
    leaf(work, upper, inverse)
    factor_ref[0:128, 0:128] = upper[...] * (1.0 / scale)
    first_inverse = inverse[...]
    corner = nn(first_inverse, gram_ref[0:128, 128:256])
    factor_ref[0:128, 128:256] = corner * (1.0 / scale)
    lower_right = gram_ref[128:256, 128:256] - tn(corner, corner)
    last = (row >= 124) | (lane >= 124)
    work[:, :128] = jnp.where(last, unit, lower_right)
    work[:, 128:] = unit
    padded[0:128, 0:128] = first_inverse
    leaf(work, upper, inverse)
    second_inverse = inverse[...]
    below = -nn(second_inverse, tn(corner, padded[0:128, 0:128]))
    factor_ref[128:256, 0:128] = jnp.zeros((128, 128), jnp.float32)

    loads[0].wait()
    mat[0:248] = old[0:248]
    mat[248:252] = old[248:252]
    mat[252:256] = jnp.zeros((4, mat.shape[1]), jnp.float32)
    basis[0:128] = nn(first_inverse, mat[0:128])
    basis[128:256] = nn(second_inverse, mat[128:256]) + nn(below, mat[0:128])

    cross = cross_ref[...]
    cross_left, cross_right = cross[:, :128], cross[:, 128:]
    lane8 = lax.broadcasted_iota(jnp.int32, (8, 128), 1)
    sub8 = lax.broadcasted_iota(jnp.int32, (8, 128), 0)
    inner = jnp.where(lane8 < 124, cross_right, 0.0)
    low_left = nt(cross_left, first_inverse)
    low_right = nt(cross_left, below) + nt(inner, second_inverse)
    low_right = jnp.where(lane8 < 124, low_right, 0.0)
    padded[...] = jnp.zeros_like(padded)
    padded[120:128, 0:128] = low_left
    padded[120:128, 128:256] = low_right
    low = jnp.concatenate([low_left, low_right], axis=1)
    block = cross_right - nt(low, padded[...])
    block = jnp.where((sub8 >= 4) & (lane8 >= 124), block, jnp.where(lane8 == sub8 + 120, 1.0, 0.0))
    rest = snap_ref[...] - nn(low, basis[...])
    lows, recips, rows, solved = eliminate(spread(block, 120), jnp.concatenate([block, rest], axis=1))
    sub768 = lax.broadcasted_iota(jnp.int32, rest.shape, 0)
    basis[...] = basis[...] * scale
    basis[248:256] = jnp.where(sub768 >= 4, solved[:, 128:] * scale, basis[248:256])
    turned = padded[...].T * (1.0 / scale)
    factor_ref[0:128, 128:256] = jnp.where(lane >= 124, turned[0:128], factor_ref[0:128, 128:256])
    factor_ref[128:256, 128:256] = jnp.where(lane >= 124, turned[128:256], upper[...] * (1.0 / scale))
    ending = jnp.where(lane8 >= sub8 + 120, solved[:, :128] * (1.0 / scale), 0.0)
    factor_ref[248:256, 128:256] = jnp.where(sub8 >= 4, ending, factor_ref[248:256, 128:256])

    store = pltpu.make_async_copy(basis, basis_ref, store_sem.at[0])
    store.start()
    loads[1].wait()
    again = pltpu.make_async_copy(new, out_new_ref, store_sem.at[1])
    again.start()
    store.wait()
    again.wait()


def on_device(sizes, fields, lapse_field, excision, sample_cells, old_basis):
    n_row, n_th, n_ph = sizes
    cr, ct, cp = lapse_field.shape
    columns = old_basis.shape[1]
    f32 = jnp.float32
    half = n_row * n_ph // 2
    rows = 256 // (2 * half)
    cells = sample_cells.reshape(cr, ct)
    vmem = pltpu.VMEM
    new_fields, gram, cross, snap = pl.pallas_call(
        functools.partial(comm_kernel, sizes),
        out_shape=(
            jax.ShapeDtypeStruct(fields.shape, f32),
            jax.ShapeDtypeStruct((256, 256), f32),
            jax.ShapeDtypeStruct((8, 256), f32),
            jax.ShapeDtypeStruct((8, columns), f32),
        ),
        in_specs=[ANY] * 5,
        out_specs=(ANY, VMEM, VMEM, VMEM),
        scratch_shapes=[
            vmem(fields.shape, f32),
            vmem(lapse_field.shape, f32),
            vmem(excision.shape, jnp.int32),
            vmem(cells.shape, jnp.int32),
            vmem(old_basis.shape, f32),
            vmem((256, columns), f32),
            vmem(fields.shape, f32),
            vmem(fields.shape, f32),
            vmem(lapse_field.shape, f32),
            vmem((2, 6, cr * ct, cp), f32),
            vmem((2, 6, cr + 4, 32, cp), f32),
            vmem((2, 2, 4, 2, cr, cp), f32),
            vmem((2, 2, 4, 2, cr, cp), f32),
            vmem((2, 2, ct, cp), f32),
            vmem((2, 2, ct, cp), f32),
            vmem((2 * half, rows, 256), f32),
            vmem((2 * half, rows, 256), f32),
            vmem((half, rows, 256), f32),
            vmem((half - 1, rows, 256), f32),
            vmem((n_th, rows, 256), f32),
            vmem((2 * half, 8, 256), f32),
            vmem((n_th, 8, 256), f32),
            pltpu.SemaphoreType.DMA((5,)),
            pltpu.SemaphoreType.DMA,
            pltpu.SemaphoreType.DMA((2, 6)),
            pltpu.SemaphoreType.DMA((2, 6)),
            pltpu.SemaphoreType.DMA((7,)),
            pltpu.SemaphoreType.DMA((7,)),
        ],
        compiler_params=pltpu.CompilerParams(
            collective_id=0, has_side_effects=True, vmem_limit_bytes=48 * 1024 * 1024
        ),
        name="halo_and_gram",
    )(fields, lapse_field, excision, cells, old_basis)
    total_rows = columns * n_row * n_th * n_ph
    return pl.pallas_call(
        functools.partial(solve_kernel, math.sqrt(total_rows)),
        out_shape=(
            jax.ShapeDtypeStruct(fields.shape, f32),
            jax.ShapeDtypeStruct((256, columns), f32),
            jax.ShapeDtypeStruct((256, 256), f32),
        ),
        in_specs=[VMEM, VMEM, VMEM, ANY, ANY],
        out_specs=(ANY, ANY, VMEM),
        scratch_shapes=[
            vmem(fields.shape, f32),
            vmem(old_basis.shape, f32),
            vmem((256, columns), f32),
            vmem((128, 256), f32),
            vmem((128, 128), f32),
            vmem((128, 128), f32),
            vmem((256, columns), f32),
            vmem((128, 256), f32),
            pltpu.SemaphoreType.DMA((2,)),
            pltpu.SemaphoreType.DMA((2,)),
        ],
        compiler_params=pltpu.CompilerParams(vmem_limit_bytes=32 * 1024 * 1024),
        name="factor_and_solve",
    )(gram, cross, snap, old_basis, new_fields)


def solution(mesh):
    sizes = tuple(mesh.shape[name] for name in ("row", "th", "ph"))
    return jax.shard_map(
        functools.partial(on_device, sizes),
        mesh=mesh,
        in_specs=(
            P(None, "row", "th", "ph"),
            P("row", "th", "ph"),
            P("row", "th", "ph"),
            P("row", "th", "ph"),
            P(None, ("row", "th", "ph")),
        ),
        out_specs=(P(None, "row", "th", "ph"), P(None, ("row", "th", "ph")), P()),
        check_vma=False,
    )
```

time: 413 us -> 58.2 us (0.14)
  waiting for transfers between devices: 280 us -> 0 us
  other arithmetic: 67.8 us -> 0 us
  Pallas kernels: 0 us -> 51.9 us
  starting transfers between devices: 31.9 us -> 0 us
  between operations: 15.7 us -> 0.81 us
  local copies, waits for them, and re-layouts: 12.8 us -> 4.76 us
    psum x1 -> x0, waiting for transfers between devices: 254 us -> none  [on_device(): lax.psum(jnp.dot(matrix, matrix.T, precision=lax.Precision.HIGHEST), ('ro...]
    another operation x16 -> x0, other arithmetic: 58 us -> none  [the longest x7 34.6 us: on_device(): factor_low = lax.linalg.cholesky(gram_sum)]
    pallas_call x0 -> x2, Pallas kernels: none -> 51.9 us  [the longest x1 38.2 us: on_device(): pl.pallas_call(functools.partial(comm_kernel, sizes), out_shape=(jax.Shap...]
    ppermute x12 -> x0, starting transfers between devices: 31.8 us -> none  [the longest x6 22.4 us: with_halo(): lax.ppermute(lax.slice_in_dim(block, block.shape[dim] - width, None, axis...]
    ppermute x12 -> x0, waiting for transfers between devices: 25.3 us -> none  [the longest x6 18.2 us: with_halo(): lax.ppermute(lax.slice_in_dim(block, 0, width, axis=dim), axis, backward)]
    another operation x13 -> x0, local copies, waits for them, and re-layouts: 4.44 us -> none
  transfers between devices with their start and end apart: 13 -> 0, of which waited for: 12 -> 0; matrix products, arithmetic and copies ran while one was open for 1% -> 0% of each run, Pallas kernels for 0% -> 0%
where the time goes in v1:
time: 58.2 us; the launch traced here: 57.5 us
  Pallas kernels  51.9 us (89%)
  local copies, waits for them, and re-layouts  4.76 us (8%)
  between operations  0.81 us (1%)
    pallas_call x1, Pallas kernels, on_device(): pl.pallas_call(functools.partial(comm_kernel, sizes), out_shape=(jax.Shap...  38.2 us
    pallas_call x1, Pallas kernels, on_device(): pl.pallas_call(functools.partial(solve_kernel, math.sqrt(total_rows)), ou...  13.7 us
    unnamed x10, local copies, waits for them, and re-layouts  4.76 us

profile of v1, /device:TPU:1, one launch (start us, length us, event | category | flops | bytes accessed | tf_op | source)
XLA Modules:
  0.0 57.5 jit_solution(9351147628291386498)
XLA Ops:
  0.6 0.0 copy-start
  0.6 1.1 %copy-done = f32[252,768]{1,0:T(8,128)S(1)} copy-done((f32[252,768]{1,0:T(8,128)S(1)}, f32[252,768]{1,0:T(8,128)}, u32[]{:S(2)}) %copy-start) | copy-done | bytes 774168
  1.8 0.0 copy-start.1
  1.8 1.1 %copy-done.1 = f32[6,16,16,128]{3,2,1,0:T(8,128)S(1)} copy-done((f32[6,16,16,128]{3,2,1,0:T(8,128)S(1)}, f32[6,16,16,128]{3,2,1,0:T(8,128)}, u32[]{:S(2)}) %copy-start.1) | copy-done | bytes 786456
  2.9 0.0 copy-start.2
  2.9 0.9 %copy-done.2 = f32[16,16,128]{2,1,0:T(8,128)S(1)} copy-done((f32[16,16,128]{2,1,0:T(8,128)S(1)}, f32[16,16,128]{2,1,0:T(8,128)}, u32[]{:S(2)}) %copy-start.2) | copy-done | bytes 131096
  3.8 0.0 copy-start.3
  3.8 0.9 %copy-done.3 = s32[16,16,128]{2,1,0:T(8,128)S(1)} copy-done((s32[16,16,128]{2,1,0:T(8,128)S(1)}, s32[16,16,128]{2,1,0:T(8,128)}, u32[]{:S(2)}) %copy-start.3) | copy-done | bytes 131096
  4.7 0.0 copy-start.4
  4.7 0.7 %copy-done.4 = s32[16,16,1]{1,2,0:T(1,128)S(1)} copy-done((s32[16,16,1]{1,2,0:T(1,128)S(1)}, s32[16,16,1]{1,2,0:T(1,128)}, u32[]{:S(2)}) %copy-start.4) | copy-done | bytes 1048
  5.4 38.2 %halo_and_gram.1 = (f32[6,16,16,128]{3,2,1,0:T(8,128)S(1)}, f32[256,256]{1,0:T(8,128)S(1)}, f32[8,256]{1,0:T(8,128)S(1)}, f32[8,768]{1,0:T(8,128)S(1)}) custom-call(f32[6,16,16,128]{3,2,1,0:T(8,128)S(1)} %copy-done.1, f32[16,16,128]{2,1,0:T(8,128)S(1)} %copy-done.2, s32[16,16,128]{2,1,0:T(8,128)S(1)} %copy-done.3, s32[16,16]{1,0:T(8,128)S(1)} %bitcast.1, ...), custom_call_target="tpu_custom_call" | custom-call | tf_op jit(solution)/shard_map/halo_and_gram/pallas_call | solution.py:471
  43.6 13.7 %factor_and_solve.1 = (f32[6,16,16,128]{3,2,1,0:T(8,128)}, f32[256,768]{1,0:T(8,128)}, f32[256,256]{1,0:T(8,128)}) custom-call(f32[256,256]{1,0:T(8,128)S(1)} %get-tuple-element.7.gram_ref, f32[8,256]{1,0:T(8,128)S(1)} %get-tuple-element.8.cross_ref, f32[8,768]{1,0:T(8,128)S(1)} %get-tuple-element.9.snap_ref, f32[252,768]{1,0:T(8,128)S(1)} %copy-done, ...), custom_call_target="tpu_custom_call" | custom-call | tf_op jit(solution)/shard_map/factor_and_solve/pallas_call | solution.py:517
Async XLA Ops:
  0.6 1.1 %copy-start = (f32[252,768]{1,0:T(8,128)S(1)}, f32[252,768]{1,0:T(8,128)}, u32[]{:S(2)}) copy-start(f32[252,768]{1,0:T(8,128)} %old_ref.3) | copy-start | bytes 2322436
  1.8 1.1 %copy-start.1 = (f32[6,16,16,128]{3,2,1,0:T(8,128)S(1)}, f32[6,16,16,128]{3,2,1,0:T(8,128)}, u32[]{:S(2)}) copy-start(f32[6,16,16,128]{3,2,1,0:T(8,128)} %fields_ref.1) | copy-start | bytes 2359300
  2.9 0.9 %copy-start.2 = (f32[16,16,128]{2,1,0:T(8,128)S(1)}, f32[16,16,128]{2,1,0:T(8,128)}, u32[]{:S(2)}) copy-start(f32[16,16,128]{2,1,0:T(8,128)} %lapse_ref.1) | copy-start | bytes 393220
  3.8 0.9 %copy-start.3 = (s32[16,16,128]{2,1,0:T(8,128)S(1)}, s32[16,16,128]{2,1,0:T(8,128)}, u32[]{:S(2)}) copy-start(s32[16,16,128]{2,1,0:T(8,128)} %excision_ref.1) | copy-start | bytes 393220
  4.7 0.7 %copy-start.4 = (s32[16,16,1]{1,2,0:T(1,128)S(1)}, s32[16,16,1]{1,2,0:T(1,128)}, u32[]{:S(2)}) copy-start(s32[16,16,1]{1,2,0:T(1,128)} %param.8) | copy-start | bytes 3076

commit v2 on v0

v2 whole, which is shorter than its diff:
```python
import functools
import math

import jax
import jax.numpy as jnp
from jax import lax
from jax.experimental import pallas as pl
from jax.experimental.pallas import tpu as pltpu
from jax.sharding import PartitionSpec as P

MESH = pl.DeviceIdType.MESH
LIMIT = 63 * 1024 * 1024
UNROLL = 2
HIGH = lax.Precision.HIGHEST
VMEM = pl.BlockSpec(memory_space=pltpu.VMEM)
HBM = pl.BlockSpec(memory_space=pltpu.HBM)

damping_rate = 3.0
time_step = 0.3
azimuth_gain = 5.0

SLOT = {0: 0, 3: 1, 2: 2, 5: 3, 1: 4, 4: 5}
EDGE = {0: 0, 3: 1, 1: 2, 4: 3}


def nt(a, b):
    return lax.dot_general(a, b, (((1,), (1,)), ((), ())), precision=HIGH, preferred_element_type=jnp.float32)


def nn(a, b):
    return lax.dot_general(a, b, (((1,), (0,)), ((), ())), precision=HIGH, preferred_element_type=jnp.float32)


def tn(a, b):
    return lax.dot_general(a, b, (((0,), (0,)), ((), ())), precision=HIGH, preferred_element_type=jnp.float32)


def diff(near_high, near_low, far_high, far_low, gain):
    return (8.0 * (near_high - near_low) - (far_high - far_low)) * (gain / 12.0)


def sublane(x, k):
    return jnp.broadcast_to(x[k : k + 1], x.shape)


def eliminate(columns, x, follower=None):
    sub = lax.broadcasted_iota(jnp.int32, x.shape, 0)
    columns = list(columns)
    lows, recips, rows = [], [], []
    solved = jnp.zeros_like(x)
    for k in range(8):
        recip = lax.rsqrt(sublane(columns[k], k))
        low = columns[k] * recip
        for b in range(k + 1, 8):
            columns[b] = columns[b] - low * sublane(low, b)
        wide = jnp.tile(recip, (1, x.shape[1] // 128))
        line = sublane(x, k) * wide
        x = x - jnp.tile(low, (1, x.shape[1] // 128)) * line
        solved = jnp.where(sub == k, line, solved)
        lows.append(low)
        recips.append(recip)
        rows.append(line)
        if follower is not None:
            follower(k, recip, low, line)
    return lows, recips, rows, solved


def spread(tile, first):
    return [jnp.broadcast_to(tile[:, first + b : first + b + 1], (8, 128)) for b in range(8)]


def twice(x):
    return jnp.concatenate([x, x], axis=1)


def leaf(work, upper, inverse):
    for p in range(16):
        r0 = 8 * p
        x = work[r0 : r0 + 8]
        state = {}
        if p < 15:
            state["x"] = work[r0 + 8 : r0 + 16]
            state["e"] = spread(state["x"], r0)

        def follower(k, recip, low, line):
            mine = state["e"][k] * recip
            state["x"] = state["x"] - twice(mine) * line
            for b in range(k + 1, 8):
                state["e"][b] = state["e"][b] - mine * sublane(low, b)

        lows, recips, rows, solved = eliminate(spread(x, r0), x, follower if p < 15 else None)
        lane = lax.broadcasted_iota(jnp.int32, (8, 128), 1)
        sub = lax.broadcasted_iota(jnp.int32, (8, 128), 0)
        upper[r0 : r0 + 8] = jnp.where(lane >= sub + r0, solved[:, :128], 0.0)
        inverse[r0 : r0 + 8] = solved[:, 128:]
        if p < 15:
            work[r0 + 8 : r0 + 16] = state["x"]
        if p < 14:
            back = [None] * 8
            for q in range(7, -1, -1):
                value = rows[q]
                for a in range(q + 1, 8):
                    value = value - twice(sublane(lows[q], a)) * back[a]
                back[q] = value * twice(recips[q])
            for t in range(p + 2, 16):
                tile = work[8 * t : 8 * t + 8]
                for k, column in enumerate(spread(tile, r0)):
                    tile = tile - twice(column) * back[k]
                work[8 * t : 8 * t + 8] = tile


def comm_kernel(
    sizes, scale,
    fields_ref, lapse_ref, excision_ref, cells_ref, old_ref,
    new_ref, inverse_ref, factor_ref, matrix_ref,
    field, lapse, excision, cells, old, mat, fresh, section, weighted, masked0, masked1,
    padded0, padded1, polar_out0, polar_out1, polar_in0, polar_in1, edge_out0, edge_out1, edge_in0, edge_in1,
    gram, full, pair, plane, deep, cross_pair, cross_plane, cross_deep, inv, fac,
    work, factor_block, upper, inverse, padded_low,
    load_sem, store_sem, halo_send, halo_recv, send_sem, recv_sem,
):
    masked, padded = (masked0, masked1), (padded0, padded1)
    polar_out, polar_in = (polar_out0, polar_out1), (polar_in0, polar_in1)
    edge_out, edge_in = (edge_out0, edge_out1), (edge_in0, edge_in1)
    n_row, n_th, n_ph = sizes
    n_y = n_row // 2
    row, th, ph = lax.axis_index("row"), lax.axis_index("th"), lax.axis_index("ph")
    core, y = lax.rem(row, 2), lax.div(row, 2)
    spot = y * n_ph + ph
    half = n_y * n_ph
    chunks = 2 * half
    owner = core * half + spot
    cr, ct, cp = 16, 16, 128

    loads = [
        pltpu.make_async_copy(source, target, load_sem.at[k])
        for k, (source, target) in enumerate(
            ((old_ref, old), (fields_ref, field), (lapse_ref, lapse), (excision_ref, excision), (cells_ref, cells))
        )
    ]
    for load in loads:
        load.start()

    def place(index):
        which, rest = lax.div(index, half), lax.rem(index, half)
        return {"row": lax.div(rest, n_ph) * 2 + which, "ph": lax.rem(rest, n_ph)}

    def in_plane(d):
        return place(lax.rem(owner + d, chunks))

    def in_half(d):
        return place(core * half + lax.rem(spot + d, half))

    def along(d):
        return {"th": lax.rem(th + d, n_th)}

    barrier = pltpu.get_barrier_semaphore()
    for d in range(1, chunks):
        pl.semaphore_signal(barrier, inc=1, device_id=in_plane(d), device_id_type=MESH)
    for d in range(1, n_th):
        pl.semaphore_signal(barrier, inc=1, device_id=along(d), device_id_type=MESH)

    def send(source, target, device, k):
        copy = pltpu.make_async_remote_copy(
            src_ref=source, dst_ref=target, send_sem=send_sem.at[k], recv_sem=recv_sem.at[k],
            device_id=device, device_id_type=MESH,
        )
        copy.start()

    def landed(ref, k):
        pltpu.make_async_copy(ref, ref, recv_sem.at[k]).wait()

    def left(ref, k):
        pltpu.make_async_copy(ref, ref, send_sem.at[k]).wait()

    lane = lax.broadcasted_iota(jnp.int32, (ct, cp), 1)
    lane_pair = lax.shift_right_logical(lane, 1)

    loads[0].wait()
    mat[0:248] = old[0:248]
    mat[248:252] = old[248:252]
    mat[252:256] = jnp.zeros((4, mat.shape[1]), jnp.float32)
    top = nt(mat[0:128], mat[0:128])
    top = jnp.concatenate([top, jnp.zeros_like(top)], axis=1)
    gram_rows = gram.shape[1]
    gram[0:half] = top.reshape(half, gram_rows, 256)
    gram[half : 2 * half] = nt(mat[128:256], mat[...]).reshape(half, gram_rows, 256)
    pl.semaphore_wait(barrier, chunks - 1 + n_th - 1)
    other = 1 - core
    send(gram.at[pl.ds(other * half, half)], pair, {"row": y * 2 + other}, 0)

    def keep_product(stage, c, i, value, edges):
        slot = SLOT[c]
        padded[stage][slot, i + 2, 8:24, :] = value
        if slot < 4:
            for s in range(2):
                polar_out[stage][0, slot, s, pl.ds(i, 1), :] = value[s : s + 1]
                polar_out[stage][1, slot, s, pl.ds(i, 1), :] = value[14 + s : 15 + s]
        if c in EDGE:
            t = EDGE[c] * cr + i
            here = lane_pair == t
            edges = (
                jnp.where(here, pltpu.roll(value, 2 * t, 1), edges[0]),
                jnp.where(here, pltpu.roll(value, (2 * t + 2) % cp, 1), edges[1]),
            )
        return edges

    def unrolled(body, carry, by=UNROLL):
        def several(k, carry):
            for u in range(by):
                carry = body(k * by + u, carry)
            return carry

        if by == cr:
            return several(0, carry)
        return lax.fori_loop(0, cr // by, several, carry)

    def sample(stage):
        for c in range(6):
            for h in range(cr * ct // cp):
                line = jnp.sum(masked[stage][c, h * cp : (h + 1) * cp, :].T, axis=0, keepdims=True)
                r, first = 252 + 2 * stage + c // 3, (c % 3) * cr * ct + h * cp
                mat[r : r + 1, first : first + cp] = line

    def at(i):
        return slice(i * ct, (i + 1) * ct) if isinstance(i, int) else pl.ds(pl.multiple_of(i * ct, ct), ct)

    def no_edges():
        return jnp.zeros((ct, cp), jnp.float32), jnp.zeros((ct, cp), jnp.float32)

    def first_products(i, edges):
        scale = lapse[i]
        for c in range(6):
            edges = keep_product(0, c, i, scale * field[c, i], edges)
        return edges

    def halo_copies(stage):
        rows = ((padded[stage].at[2:6, 2:4, 8:24, :], padded[stage].at[2:6, 18:20, 8:24, :], {"row": lax.rem(row + n_row - 1, n_row)}),
                (padded[stage].at[2:6, 16:18, 8:24, :], padded[stage].at[2:6, 0:2, 8:24, :], {"row": lax.rem(row + 1, n_row)}))
        polars = ((polar_out[stage].at[0], polar_in[stage].at[1], {"th": lax.rem(th + n_th - 1, n_th)}),
                  (polar_out[stage].at[1], polar_in[stage].at[0], {"th": lax.rem(th + 1, n_th)}))
        edges = ((edge_out[stage].at[0], edge_in[stage].at[1], {"ph": lax.rem(ph + n_ph - 1, n_ph)}),
                 (edge_out[stage].at[1], edge_in[stage].at[0], {"ph": lax.rem(ph + 1, n_ph)}))
        return [
            pltpu.make_async_remote_copy(
                src_ref=source, dst_ref=target, send_sem=halo_send.at[stage, k], recv_sem=halo_recv.at[stage, k],
                device_id=device, device_id_type=MESH,
            )
            for k, (source, target, device) in enumerate(rows + polars + edges)
        ]

    def keep_edges(stage, edges):
        edge_out[stage][0] = edges[0]
        edge_out[stage][1] = edges[1]

    for load in loads[1:]:
        load.wait()
    keep_edges(0, unrolled(first_products, no_edges(), cr))

    halos = [halo_copies(0), halo_copies(1)]
    for copy in halos[0]:
        copy.start()
    pol_index = (th * ct + lax.broadcasted_iota(jnp.int32, (ct, cp), 0)).astype(jnp.float32)
    polar = jnp.pi * (pol_index + 0.5) / (n_th * ct)
    polar_weight = jnp.sqrt(jnp.sin(polar))
    chosen = cells[...].T
    for i in range(cr):
        radius = 1.0 + 2.0 * ((row * cr + i).astype(jnp.float32) + 0.5) / (n_row * cr)
        weighted[i] = jnp.where(lane == chosen[:, i : i + 1], polar_weight * radius, 0.0)

    def rates(stage, i, c_values):
        damped = damping_rate * excision[i].astype(jnp.float32)
        lo_edge, hi_edge = edge_in[stage][0], edge_in[stage][1]
        for slot in range(4):
            for s in range(2):
                low = polar_in[stage][0, slot, s, pl.ds(i, 1), :]
                high = polar_in[stage][1, slot, s, pl.ds(i, 1), :]
                padded[stage][slot, i + 2, 6 + s : 7 + s, :] = jnp.where(th > 0, low, 0.0)
                padded[stage][slot, i + 2, 24 + s : 25 + s, :] = jnp.where(th < n_th - 1, high, 0.0)

        def rad(c):
            get = lambda o: padded[stage][SLOT[c], i + 2 + o, 8:24, :]
            return diff(get(1), get(-1), get(2), get(-2), 1.0)

        def pol(c):
            get = lambda o: padded[stage][SLOT[c], i + 2, 8 + o : 24 + o, :]
            return diff(get(1), get(-1), get(2), get(-2), 1.0)

        def azi(c):
            here = padded[stage][SLOT[c], i + 2, 8:24, :]
            t = EDGE[c] * cr + i
            low = pltpu.roll(lo_edge, cp - 2 - 2 * t, 1)
            high = pltpu.roll(hi_edge, (cp - 2 * t) % cp, 1)
            far_low = pltpu.roll(jnp.where(lane >= cp - 2, low, here), 2, 1)
            near_low = pltpu.roll(jnp.where(lane >= cp - 1, low, here), 1, 1)
            near_high = pltpu.roll(jnp.where(lane < 1, high, here), cp - 1, 1)
            far_high = pltpu.roll(jnp.where(lane < 2, high, here), cp - 2, 1)
            return diff(near_high, near_low, far_high, far_low, azimuth_gain)

        out = []
        for start, sign in ((3, 1.0), (0, -1.0)):
            curls = (pol(start + 2) - azi(start + 1), azi(start) - rad(start + 2), rad(start + 1) - pol(start))
            for k in range(3):
                c = len(out)
                out.append((curls[k] if sign > 0 else -curls[k]) - damped * c_values[c])
        return out

    def zero_ends(stage):
        low = padded[stage][2:6, 0:2, 8:24, :]
        padded[stage][2:6, 0:2, 8:24, :] = jnp.where(row > 0, low, 0.0)
        high = padded[stage][2:6, 18:20, 8:24, :]
        padded[stage][2:6, 18:20, 8:24, :] = jnp.where(row < n_row - 1, high, 0.0)

    def first_step(i, edges):
        values = [field[c, i] for c in range(6)]
        rate = rates(0, i, values)
        scale, pick = lapse[i], weighted[i]
        for c in range(6):
            value = values[c] + time_step * rate[c]
            section[c, i] = value
            masked[0][c, at(i), :] = value * pick
            edges = keep_product(1, c, i, scale * value, edges)
        return edges

    def second_step(i, nothing):
        values = [section[c, i] for c in range(6)]
        rate = rates(1, i, values)
        pick = weighted[i]
        for c in range(6):
            value = 0.5 * (field[c, i] + values[c] + time_step * rate[c])
            fresh[c, i] = value
            masked[1][c, at(i), :] = value * pick
        return nothing

    landed(pair, 0)
    mine = pl.ds(core * half, half)
    gram[mine] = gram[mine] + pair[...]
    for d in range(1, half):
        send(gram.at[core * half + lax.rem(spot + d, half)], plane.at[d - 1], in_half(d), 1)

    for copy in halos[0]:
        copy.wait_recv()
    zero_ends(0)
    keep_edges(1, unrolled(first_step, no_edges()))
    for copy in halos[1]:
        copy.start()
    sample(0)

    landed(plane, 1)
    total = gram[owner]
    for d in range(1, half):
        total = total + plane[d - 1]
    deep[0] = total
    for d in range(1, n_th):
        send(deep.at[0], deep.at[d], along(d), 2)

    for copy in halos[1]:
        copy.wait_recv()
    zero_ends(1)
    unrolled(second_step, 0)
    landed(deep.at[1:], 2)
    total = deep[th]
    for a in range(1, n_th):
        total = total + deep[lax.rem(th - a + n_th, n_th)]
    full[owner] = total
    for d in range(1, half):
        send(full.at[owner], full.at[owner], in_half(d), 4)

    stores = [pltpu.make_async_copy(fresh, new_ref, store_sem.at[0])]
    stores[0].start()
    sample(1)
    stores.append(pltpu.make_async_copy(mat, matrix_ref, store_sem.at[1]))
    stores[1].start()
    place_row = lax.broadcasted_iota(jnp.int32, (8, mat.shape[1]), 0)
    snap = jnp.where(place_row >= 4, mat[248:256], 0.0)
    cross_pair[core] = nt(snap, mat[...])[4:8]
    send(cross_pair.at[core], cross_pair.at[core], {"row": y * 2 + other}, 3)
    landed(cross_pair.at[0], 3)
    cross_plane[0] = cross_pair[0] + cross_pair[1]
    for d in range(1, half):
        send(cross_plane.at[0], cross_plane.at[d], in_half(d), 7)

    landed(plane, 4)
    send(full.at[mine], full.at[mine], {"row": y * 2 + other}, 6)
    square = lax.broadcasted_iota(jnp.int32, (128, 128), 0)
    column = lax.broadcasted_iota(jnp.int32, (128, 128), 1)
    unit = (square == column).astype(jnp.float32)
    inv[0:128, 128:256] = jnp.zeros((128, 128), jnp.float32)
    fac[128:256, 0:128] = jnp.zeros((128, 128), jnp.float32)
    padded_low[...] = jnp.zeros_like(padded_low)
    landed(pair, 6)
    gram_half = chunks // 2
    top = full[0:gram_half].reshape(128, 256)
    bottom = full[gram_half:chunks].reshape(128, 256)
    work[:, :128] = top[:, :128]
    work[:, 128:] = unit
    upper[...] = bottom[:, :128]

    def block(b, nothing):
        leaf(work, factor_block, inverse)

        @pl.when(b == 0)
        def _():
            first = inverse[...]
            inv[0:128, 0:128] = first
            fac[0:128, 0:128] = factor_block[...] * (1.0 / scale)
            corner = nt(first, upper[...])
            upper[...] = corner
            last = (square >= 124) | (column >= 124)
            right = full[gram_half:chunks].reshape(128, 256)[:, 128:]
            work[:, :128] = jnp.where(last, unit, right - tn(corner, corner))
            work[:, 128:] = unit
            landed(cross_plane.at[1:], 7)
            total = cross_plane[spot]
            for a in range(1, half):
                total = total + cross_plane[lax.rem(spot - a + half, half)]
            cross_deep[0] = total
            for d in range(1, n_th):
                send(cross_deep.at[0], cross_deep.at[d], along(d), 5)

        return nothing

    lax.fori_loop(0, 2, block, 0)

    second = inverse[...]
    first = inv[0:128, 0:128]
    corner = upper[...]
    below = -nn(second, tn(corner, first))
    inv[128:256, 0:128] = below
    inv[128:256, 128:256] = second

    landed(cross_deep.at[1:], 5)
    cross = cross_deep[th]
    for a in range(1, n_th):
        cross = cross + cross_deep[lax.rem(th - a + n_th, n_th)]
    cross = jnp.concatenate([jnp.zeros((4, 256), jnp.float32), cross], axis=0)
    cross_left, cross_right = cross[:, :128], cross[:, 128:]
    lane8 = lax.broadcasted_iota(jnp.int32, (8, 128), 1)
    sub8 = lax.broadcasted_iota(jnp.int32, (8, 128), 0)
    inner = jnp.where(lane8 < 124, cross_right, 0.0)
    low_left = nt(cross_left, first)
    low_right = jnp.where(lane8 < 124, nt(cross_left, below) + nt(inner, second), 0.0)
    padded_low[120:128, 0:128] = low_left
    padded_low[120:128, 128:256] = low_right
    low = jnp.concatenate([low_left, low_right], axis=1)
    snapshot_block = cross_right - nt(low, padded_low[...])
    real = sub8 >= 4
    diagonal = (lane8 == sub8 + 120).astype(jnp.float32)
    snapshot_block = jnp.where(real & (lane8 >= 124), snapshot_block, diagonal)
    rest_left = -(nn(low_left, first) + nn(low_right, below))
    rest_right = diagonal - nn(low_right, second)
    _, _, _, solved = eliminate(
        spread(snapshot_block, 120), jnp.concatenate([snapshot_block, rest_left, rest_right], axis=1)
    )
    real_wide = lax.broadcasted_iota(jnp.int32, (8, 256), 0) >= 4
    inv[248:256] = jnp.where(real_wide, solved[:, 128:], inv[248:256])
    turned = padded_low[...].T
    fac[0:128, 128:256] = jnp.where(column >= 124, turned[0:128], corner) * (1.0 / scale)
    fac[128:256, 128:256] = jnp.where(column >= 124, turned[128:256], factor_block[...]) * (1.0 / scale)
    finish = jnp.where(lane8 >= sub8 + 120, solved[:, :128] * (1.0 / scale), 0.0)
    fac[248:256, 128:256] = jnp.where(real, finish, fac[248:256, 128:256])

    stores.append(pltpu.make_async_copy(inv, inverse_ref, store_sem.at[2]))
    stores.append(pltpu.make_async_copy(fac, factor_ref, store_sem.at[3]))
    for store in stores[2:]:
        store.start()
    for stage in range(2):
        for copy in halos[stage]:
            copy.wait_send()
    left(pair, 0)
    left(plane, 1)
    left(deep.at[1:], 2)
    left(cross_pair.at[0], 3)
    left(cross_plane.at[1:], 7)
    left(plane, 4)
    left(cross_deep.at[1:], 5)
    left(pair, 6)
    for store in stores:
        store.wait()


def apply_kernel(
    scale,
    new_ref, inverse_ref, factor_ref, matrix_ref,
    out_new_ref, basis_ref, out_factor_ref,
    inverse, matrix, new, factor, basis, load_sem, sem,
):
    def pieces(source, target, count):
        rows = source.shape[0] // count
        return [(source.at[k * rows : (k + 1) * rows], target.at[k * rows : (k + 1) * rows]) for k in range(count)]

    loads = pieces(inverse_ref, inverse, 2) + pieces(matrix_ref, matrix, 2) + [(factor_ref, factor), (new_ref, new)]
    loads = [pltpu.make_async_copy(source, target, load_sem.at[k]) for k, (source, target) in enumerate(loads)]
    for load in loads:
        load.start()
    copies = []
    for h in range(2):
        rows = slice(128 * h, 128 * h + 128)
        loads[h].wait()
        loads[2 + h].wait()
        basis[rows] = nn(inverse[rows, : 128 * h + 128], matrix[: 128 * h + 128]) * scale
        copies.append(pltpu.make_async_copy(basis.at[rows], basis_ref.at[rows], sem.at[h]))
        copies[-1].start()
        if h == 0:
            for k, source, target in ((4, factor, out_factor_ref), (5, new, out_new_ref)):
                loads[k].wait()
                copies.append(pltpu.make_async_copy(source, target, sem.at[k - 2]))
                copies[-1].start()
    for copy in copies:
        copy.wait()


def on_device(sizes, fields, lapse_field, excision, sample_cells, old_basis):
    n_row, n_th, n_ph = sizes
    cr, ct, cp = lapse_field.shape
    columns = old_basis.shape[1]
    f32 = jnp.float32
    half = n_row * n_ph // 2
    rows = 256 // (2 * half)
    cells = sample_cells.reshape(cr, ct)
    vmem = pltpu.VMEM
    scale = math.sqrt(columns * n_row * n_th * n_ph)
    between = (
        jax.ShapeDtypeStruct(fields.shape, f32),
        jax.ShapeDtypeStruct((256, 256), f32),
        jax.ShapeDtypeStruct((256, 256), f32),
        jax.ShapeDtypeStruct((256, columns), f32),
    )
    between = pl.pallas_call(
        functools.partial(comm_kernel, sizes, scale),
        out_shape=between,
        in_specs=[HBM] * 5,
        out_specs=(HBM,) * 4,
        scratch_shapes=[
            vmem(fields.shape, f32),
            vmem(lapse_field.shape, f32),
            vmem(excision.shape, jnp.int32),
            vmem(cells.shape, jnp.int32),
            vmem(old_basis.shape, f32),
            vmem((256, columns), f32),
            vmem(fields.shape, f32),
            vmem(fields.shape, f32),
            vmem(lapse_field.shape, f32),
            vmem((6, cr * ct, cp), f32),
            vmem((6, cr * ct, cp), f32),
            vmem((6, cr + 4, 32, cp), f32),
            vmem((6, cr + 4, 32, cp), f32),
            vmem((2, 4, 2, cr, cp), f32),
            vmem((2, 4, 2, cr, cp), f32),
            vmem((2, 4, 2, cr, cp), f32),
            vmem((2, 4, 2, cr, cp), f32),
            vmem((2, ct, cp), f32),
            vmem((2, ct, cp), f32),
            vmem((2, ct, cp), f32),
            vmem((2, ct, cp), f32),
            vmem((2 * half, rows, 256), f32),
            vmem((2 * half, rows, 256), f32),
            vmem((half, rows, 256), f32),
            vmem((half - 1, rows, 256), f32),
            vmem((n_th, rows, 256), f32),
            vmem((2, 4, 256), f32),
            vmem((half, 4, 256), f32),
            vmem((n_th, 4, 256), f32),
            vmem((256, 256), f32),
            vmem((256, 256), f32),
            vmem((128, 256), f32),
            vmem((128, 128), f32),
            vmem((128, 128), f32),
            vmem((128, 128), f32),
            vmem((128, 256), f32),
            pltpu.SemaphoreType.DMA((5,)),
            pltpu.SemaphoreType.DMA((4,)),
            pltpu.SemaphoreType.DMA((2, 6)),
            pltpu.SemaphoreType.DMA((2, 6)),
            pltpu.SemaphoreType.DMA((8,)),
            pltpu.SemaphoreType.DMA((8,)),
        ],
        compiler_params=pltpu.CompilerParams(
            collective_id=0, has_side_effects=True, vmem_limit_bytes=LIMIT
        ),
        name="halo_and_gram",
    )(fields, lapse_field, excision, cells, old_basis)
    return pl.pallas_call(
        functools.partial(apply_kernel, scale),
        out_shape=(
            jax.ShapeDtypeStruct(fields.shape, f32),
            jax.ShapeDtypeStruct((256, columns), f32),
            jax.ShapeDtypeStruct((256, 256), f32),
        ),
        in_specs=[HBM] * 4,
        out_specs=(HBM,) * 3,
        scratch_shapes=[
            vmem((256, 256), f32),
            vmem((256, columns), f32),
            vmem(fields.shape, f32),
            vmem((256, 256), f32),
            vmem((256, columns), f32),
            pltpu.SemaphoreType.DMA((6,)),
            pltpu.SemaphoreType.DMA((4,)),
        ],
        compiler_params=pltpu.CompilerParams(vmem_limit_bytes=LIMIT),
        name="apply",
    )(*between)


def solution(mesh):
    sizes = tuple(mesh.shape[name] for name in ("row", "th", "ph"))
    return jax.shard_map(
        functools.partial(on_device, sizes),
        mesh=mesh,
        in_specs=(
            P(None, "row", "th", "ph"),
            P("row", "th", "ph"),
            P("row", "th", "ph"),
            P("row", "th", "ph"),
            P(None, ("row", "th", "ph")),
        ),
        out_specs=(P(None, "row", "th", "ph"), P(None, ("row", "th", "ph")), P()),
        check_vma=False,
    )
```

time: 413 us -> 46.4 us (0.11)
  waiting for transfers between devices: 280 us -> 0 us
  other arithmetic: 67.8 us -> 0 us
  Pallas kernels: 0 us -> 45.7 us
  starting transfers between devices: 31.9 us -> 0 us
  between operations: 15.7 us -> 0.64 us
  local copies, waits for them, and re-layouts: 12.8 us -> 0 us
    psum x1 -> x0, waiting for transfers between devices: 254 us -> none  [on_device(): lax.psum(jnp.dot(matrix, matrix.T, precision=lax.Precision.HIGHEST), ('ro...]
    another operation x16 -> x0, other arithmetic: 58 us -> none  [the longest x7 34.6 us: on_device(): factor_low = lax.linalg.cholesky(gram_sum)]
    pallas_call x0 -> x2, Pallas kernels: none -> 45.7 us  [the longest x1 42.5 us: on_device(): pl.pallas_call(functools.partial(comm_kernel, sizes, scale), out_shape=be...]
    ppermute x12 -> x0, starting transfers between devices: 31.8 us -> none  [the longest x6 22.4 us: with_halo(): lax.ppermute(lax.slice_in_dim(block, block.shape[dim] - width, None, axis...]
    ppermute x12 -> x0, waiting for transfers between devices: 25.3 us -> none  [the longest x6 18.2 us: with_halo(): lax.ppermute(lax.slice_in_dim(block, 0, width, axis=dim), axis, backward)]
    another operation x13 -> x0, local copies, waits for them, and re-layouts: 4.44 us -> none
  transfers between devices with their start and end apart: 13 -> 0, of which waited for: 12 -> 0; matrix products, arithmetic and copies ran while one was open for 1% -> 0% of each run, Pallas kernels for 0% -> 0%
where the time goes in v2:
time: 46.4 us; the launch traced here: 46.3 us
  Pallas kernels  45.7 us (98%)
  between operations  0.64 us (1%)
    pallas_call x1, Pallas kernels, on_device(): pl.pallas_call(functools.partial(comm_kernel, sizes, scale), out_shape=be...  42.5 us
    pallas_call x1, Pallas kernels, on_device(): pl.pallas_call(functools.partial(apply_kernel, scale), out_shape=(jax.Sha...  3.12 us

profile of v2, /device:TPU:1, one launch (start us, length us, event | category | flops | bytes accessed | tf_op | source)
XLA Modules:
  0.0 46.3 jit_solution(13382318617858450051)
XLA Ops:
  0.6 42.5 %halo_and_gram.1 = (f32[6,16,16,128]{3,2,1,0:T(8,128)}, f32[256,256]{1,0:T(8,128)}, f32[256,256]{1,0:T(8,128)}, f32[256,768]{1,0:T(8,128)}) custom-call(f32[6,16,16,128]{3,2,1,0:T(8,128)} %fields_ref.1, f32[16,16,128]{2,1,0:T(8,128)} %lapse_ref.1, s32[16,16,128]{2,1,0:T(8,128)} %excision_ref.1, s32[16,16]{1,0:T(8,128)} %bitcast.1, f32[252,768]{1,0:T(8,128)} %old_ref.1), custom_call_target="tpu_custom_call" | custom-call | tf_op jit(solution)/shard_map/halo_and_gram/pallas_call | solution.py:529
  43.2 3.1 %apply.1 = (f32[6,16,16,128]{3,2,1,0:T(8,128)}, f32[256,768]{1,0:T(8,128)}, f32[256,256]{1,0:T(8,128)}) custom-call(f32[6,16,16,128]{3,2,1,0:T(8,128)} %get-tuple-element.7.new_ref, f32[256,256]{1,0:T(8,128)} %get-tuple-element.8.inverse_ref, f32[256,256]{1,0:T(8,128)} %get-tuple-element.9.factor_ref, f32[256,768]{1,0:T(8,128)} %get-tuple-element.10.matrix_ref), custom_call_target="tpu_custom_call" | custom-call | tf_op jit(solution)/shard_map/apply/pallas_call | solution.py:583

commit v3 on v2

--- a/solution.py
+++ b/solution.py
@@ -12,7 +12,6 @@
 LIMIT = 63 * 1024 * 1024
 UNROLL = 2
 HIGH = lax.Precision.HIGHEST
-VMEM = pl.BlockSpec(memory_space=pltpu.VMEM)
 HBM = pl.BlockSpec(memory_space=pltpu.HBM)
 
 damping_rate = 3.0
@@ -112,11 +111,13 @@
 def comm_kernel(
     sizes, scale,
     fields_ref, lapse_ref, excision_ref, cells_ref, old_ref,
-    new_ref, inverse_ref, factor_ref, matrix_ref,
+    new_ref, basis_ref, factor_ref,
     field, lapse, excision, cells, old, mat, fresh, section, weighted, masked0, masked1,
-    padded0, padded1, polar_out0, polar_out1, polar_in0, polar_in1, edge_out0, edge_out1, edge_in0, edge_in1,
-    gram, full, pair, plane, deep, cross_pair, cross_plane, cross_deep, inv, fac,
-    work, factor_block, upper, inverse, padded_low,
+    padded0, padded1, polar_out0, polar_out1, polar_in0, polar_in1, edge_out0, edge_out1, edge_in0, edge_in1, outside,
+    first_part, first_pair, first_sum, first_plane, first_deep, first_full,
+    other_part, other_pair, other_sum, other_plane, other_deep, other_full,
+    cross_plane, cross_deep,
+    work, upper, inverse, padded_low, basis, factor,
     load_sem, store_sem, halo_send, halo_recv, send_sem, recv_sem,
 ):
     masked, padded = (masked0, masked1), (padded0, padded1)
@@ -180,30 +181,39 @@
     mat[0:248] = old[0:248]
     mat[248:252] = old[248:252]
     mat[252:256] = jnp.zeros((4, mat.shape[1]), jnp.float32)
-    top = nt(mat[0:128], mat[0:128])
-    top = jnp.concatenate([top, jnp.zeros_like(top)], axis=1)
-    gram_rows = gram.shape[1]
-    gram[0:half] = top.reshape(half, gram_rows, 256)
-    gram[half : 2 * half] = nt(mat[128:256], mat[...]).reshape(half, gram_rows, 256)
+    tiles = first_part.shape
+    first_part[...] = nt(mat[0:128], mat[0:128]).reshape(tiles)
     pl.semaphore_wait(barrier, chunks - 1 + n_th - 1)
     other = 1 - core
-    send(gram.at[pl.ds(other * half, half)], pair, {"row": y * 2 + other}, 0)
-
-    def keep_product(stage, c, i, value, edges):
+    send(first_part, first_pair, {"row": y * 2 + other}, 0)
+
+    def keep_product(stage, c, i, value):
         slot = SLOT[c]
         padded[stage][slot, i + 2, 8:24, :] = value
         if slot < 4:
             for s in range(2):
                 polar_out[stage][0, slot, s, pl.ds(i, 1), :] = value[s : s + 1]
                 polar_out[stage][1, slot, s, pl.ds(i, 1), :] = value[14 + s : 15 + s]
-        if c in EDGE:
-            t = EDGE[c] * cr + i
-            here = lane_pair == t
-            edges = (
-                jnp.where(here, pltpu.roll(value, 2 * t, 1), edges[0]),
-                jnp.where(here, pltpu.roll(value, (2 * t + 2) % cp, 1), edges[1]),
-            )
-        return edges
+
+    def keep_edges(stage):
+        low = high = jnp.zeros((ct, cp), jnp.float32)
+        for c, e in EDGE.items():
+            for i in range(cr):
+                t = e * cr + i
+                value = padded[stage][SLOT[c], i + 2, 8:24, :]
+                here = lane_pair == t
+                low = jnp.where(here, pltpu.roll(value, 2 * t, 1), low)
+                high = jnp.where(here, pltpu.roll(value, (2 * t + 2) % cp, 1), high)
+        edge_out[stage][0] = low
+        edge_out[stage][1] = high
+
+    def beyond(stage):
+        low, high = edge_in[stage][0], edge_in[stage][1]
+        for e in range(4):
+            for i in range(cr):
+                t = e * cr + i
+                moved = pltpu.roll(high, (cp - 2 * t) % cp, 1), pltpu.roll(low, cp - 2 - 2 * t, 1)
+                outside[e, i] = jnp.where(lane < cp // 2, *moved)
 
     def unrolled(body, carry, by=UNROLL):
         def several(k, carry):
@@ -225,14 +235,11 @@
     def at(i):
         return slice(i * ct, (i + 1) * ct) if isinstance(i, int) else pl.ds(pl.multiple_of(i * ct, ct), ct)
 
-    def no_edges():
-        return jnp.zeros((ct, cp), jnp.float32), jnp.zeros((ct, cp), jnp.float32)
-
-    def first_products(i, edges):
-        scale = lapse[i]
+    def first_products(i, nothing):
+        gain = lapse[i]
         for c in range(6):
-            edges = keep_product(0, c, i, scale * field[c, i], edges)
-        return edges
+            keep_product(0, c, i, gain * field[c, i])
+        return nothing
 
     def halo_copies(stage):
         rows = ((padded[stage].at[2:6, 2:4, 8:24, :], padded[stage].at[2:6, 18:20, 8:24, :], {"row": lax.rem(row + n_row - 1, n_row)}),
@@ -249,13 +256,10 @@
             for k, (source, target, device) in enumerate(rows + polars + edges)
         ]
 
-    def keep_edges(stage, edges):
-        edge_out[stage][0] = edges[0]
-        edge_out[stage][1] = edges[1]
-
     for load in loads[1:]:
         load.wait()
-    keep_edges(0, unrolled(first_products, no_edges(), cr))
+    unrolled(first_products, 0, cr)
+    keep_edges(0)
 
     halos = [halo_copies(0), halo_copies(1)]
     for copy in halos[0]:
@@ -270,7 +274,6 @@
 
     def rates(stage, i, c_values):
         damped = damping_rate * excision[i].astype(jnp.float32)
-        lo_edge, hi_edge = edge_in[stage][0], edge_in[stage][1]
         for slot in range(4):
             for s in range(2):
                 low = polar_in[stage][0, slot, s, pl.ds(i, 1), :]
@@ -288,13 +291,11 @@
 
         def azi(c):
             here = padded[stage][SLOT[c], i + 2, 8:24, :]
-            t = EDGE[c] * cr + i
-            low = pltpu.roll(lo_edge, cp - 2 - 2 * t, 1)
-            high = pltpu.roll(hi_edge, (cp - 2 * t) % cp, 1)
-            far_low = pltpu.roll(jnp.where(lane >= cp - 2, low, here), 2, 1)
-            near_low = pltpu.roll(jnp.where(lane >= cp - 1, low, here), 1, 1)
-            near_high = pltpu.roll(jnp.where(lane < 1, high, here), cp - 1, 1)
-            far_high = pltpu.roll(jnp.where(lane < 2, high, here), cp - 2, 1)
+            edge = outside[EDGE[c], i]
+            far_low = pltpu.roll(jnp.where(lane >= cp - 2, edge, here), 2, 1)
+            near_low = pltpu.roll(jnp.where(lane >= cp - 1, edge, here), 1, 1)
+            near_high = pltpu.roll(jnp.where(lane < 1, edge, here), cp - 1, 1)
+            far_high = pltpu.roll(jnp.where(lane < 2, edge, here), cp - 2, 1)
             return diff(near_high, near_low, far_high, far_low, azimuth_gain)
 
         out = []
@@ -311,16 +312,16 @@
         high = padded[stage][2:6, 18:20, 8:24, :]
         padded[stage][2:6, 18:20, 8:24, :] = jnp.where(row < n_row - 1, high, 0.0)
 
-    def first_step(i, edges):
+    def first_step(i, nothing):
         values = [field[c, i] for c in range(6)]
         rate = rates(0, i, values)
-        scale, pick = lapse[i], weighted[i]
+        gain, pick = lapse[i], weighted[i]
         for c in range(6):
             value = values[c] + time_step * rate[c]
             section[c, i] = value
             masked[0][c, at(i), :] = value * pick
-            edges = keep_product(1, c, i, scale * value, edges)
-        return edges
+            keep_product(1, c, i, gain * value)
+        return nothing
 
     def second_step(i, nothing):
         values = [section[c, i] for c in range(6)]
@@ -332,104 +333,112 @@
             masked[1][c, at(i), :] = value * pick
         return nothing
 
-    landed(pair, 0)
-    mine = pl.ds(core * half, half)
-    gram[mine] = gram[mine] + pair[...]
+    landed(first_pair, 0)
+    first_sum[...] = first_part[...] + first_pair[...]
     for d in range(1, half):
-        send(gram.at[core * half + lax.rem(spot + d, half)], plane.at[d - 1], in_half(d), 1)
-
-    for copy in halos[0]:
+        send(first_sum.at[lax.rem(spot + d, half)], first_plane.at[d - 1], in_half(d), 2)
+    remaining = nt(mat[128:256], mat[...])
+    other_part[0] = remaining[:, :128].reshape(tiles)
+    other_part[1] = remaining[:, 128:].reshape(tiles)
+    send(other_part.at[other], other_pair, {"row": y * 2 + other}, 1)
+    for copy in halos[0][4:]:
+        copy.wait_recv()
+    beyond(0)
+    landed(other_pair, 1)
+    other_sum[...] = other_part[core] + other_pair[...]
+    for d in range(1, half):
+        send(other_sum.at[lax.rem(spot + d, half)], other_plane.at[d - 1], in_half(d), 3)
+    for copy in halos[0][:4]:
         copy.wait_recv()
     zero_ends(0)
-    keep_edges(1, unrolled(first_step, no_edges()))
-    for copy in halos[1]:
+    unrolled(first_step, 0)
+    for copy in halos[1][:4]:
+        copy.start()
+    keep_edges(1)
+    for copy in halos[1][4:]:
         copy.start()
     sample(0)
 
-    landed(plane, 1)
-    total = gram[owner]
+    landed(first_plane, 2)
+    total = first_sum[spot]
     for d in range(1, half):
-        total = total + plane[d - 1]
-    deep[0] = total
+        total = total + first_plane[d - 1]
+    first_deep[0] = total
     for d in range(1, n_th):
-        send(deep.at[0], deep.at[d], along(d), 2)
-
-    for copy in halos[1]:
+        send(first_deep.at[0], first_deep.at[d], along(d), 4)
+    landed(other_plane, 3)
+    total = other_sum[spot]
+    for d in range(1, half):
+        total = total + other_plane[d - 1]
+    other_deep[0] = total
+    for d in range(1, n_th):
+        send(other_deep.at[0], other_deep.at[d], along(d), 5)
+
+    for copy in halos[1][4:]:
+        copy.wait_recv()
+    beyond(1)
+    for copy in halos[1][:4]:
         copy.wait_recv()
     zero_ends(1)
     unrolled(second_step, 0)
-    landed(deep.at[1:], 2)
-    total = deep[th]
+    landed(first_deep.at[1:], 4)
+    total = first_deep[th]
     for a in range(1, n_th):
-        total = total + deep[lax.rem(th - a + n_th, n_th)]
-    full[owner] = total
+        total = total + first_deep[lax.rem(th - a + n_th, n_th)]
+    first_full[spot] = total
     for d in range(1, half):
-        send(full.at[owner], full.at[owner], in_half(d), 4)
-
+        send(first_full.at[spot], first_full.at[spot], in_half(d), 6)
+    sample(1)
+    place_row = lax.broadcasted_iota(jnp.int32, (8, mat.shape[1]), 0)
+    snap = jnp.where(place_row >= 4, mat[248:256], 0.0)
+    cross_plane[0] = nt(snap, mat[...])[4:8]
+    for d in range(1, chunks):
+        send(cross_plane.at[0], cross_plane.at[d], in_plane(d), 9)
     stores = [pltpu.make_async_copy(fresh, new_ref, store_sem.at[0])]
     stores[0].start()
-    sample(1)
-    stores.append(pltpu.make_async_copy(mat, matrix_ref, store_sem.at[1]))
-    stores[1].start()
-    place_row = lax.broadcasted_iota(jnp.int32, (8, mat.shape[1]), 0)
-    snap = jnp.where(place_row >= 4, mat[248:256], 0.0)
-    cross_pair[core] = nt(snap, mat[...])[4:8]
-    send(cross_pair.at[core], cross_pair.at[core], {"row": y * 2 + other}, 3)
-    landed(cross_pair.at[0], 3)
-    cross_plane[0] = cross_pair[0] + cross_pair[1]
-    for d in range(1, half):
-        send(cross_plane.at[0], cross_plane.at[d], in_half(d), 7)
-
-    landed(plane, 4)
-    send(full.at[mine], full.at[mine], {"row": y * 2 + other}, 6)
     square = lax.broadcasted_iota(jnp.int32, (128, 128), 0)
     column = lax.broadcasted_iota(jnp.int32, (128, 128), 1)
     unit = (square == column).astype(jnp.float32)
-    inv[0:128, 128:256] = jnp.zeros((128, 128), jnp.float32)
-    fac[128:256, 0:128] = jnp.zeros((128, 128), jnp.float32)
+    work[:, 128:] = unit
+    factor[128:256, 0:128] = jnp.zeros((128, 128), jnp.float32)
     padded_low[...] = jnp.zeros_like(padded_low)
-    landed(pair, 6)
-    gram_half = chunks // 2
-    top = full[0:gram_half].reshape(128, 256)
-    bottom = full[gram_half:chunks].reshape(128, 256)
-    work[:, :128] = top[:, :128]
+    landed(other_deep.at[1:], 5)
+    total = other_deep[th]
+    for a in range(1, n_th):
+        total = total + other_deep[lax.rem(th - a + n_th, n_th)]
+    other_full[owner] = total
+    for d in range(1, chunks):
+        send(other_full.at[owner], other_full.at[owner], in_plane(d), 7)
+
+    landed(first_plane, 6)
+    work[:, :128] = first_full[...].reshape(128, 128)
+    leaf(work, upper, inverse)
+    landed(other_full.at[1:], 7)
+    first = inverse[...]
+    factor[0:128, 0:128] = upper[...] * (1.0 / scale)
+    corner = nt(first, other_full[0:half].reshape(128, 128))
+    last = (square >= 124) | (column >= 124)
+    work[:, :128] = jnp.where(last, unit, other_full[half:chunks].reshape(128, 128) - tn(corner, corner))
     work[:, 128:] = unit
-    upper[...] = bottom[:, :128]
-
-    def block(b, nothing):
-        leaf(work, factor_block, inverse)
-
-        @pl.when(b == 0)
-        def _():
-            first = inverse[...]
-            inv[0:128, 0:128] = first
-            fac[0:128, 0:128] = factor_block[...] * (1.0 / scale)
-            corner = nt(first, upper[...])
-            upper[...] = corner
-            last = (square >= 124) | (column >= 124)
-            right = full[gram_half:chunks].reshape(128, 256)[:, 128:]
-            work[:, :128] = jnp.where(last, unit, right - tn(corner, corner))
-            work[:, 128:] = unit
-            landed(cross_plane.at[1:], 7)
-            total = cross_plane[spot]
-            for a in range(1, half):
-                total = total + cross_plane[lax.rem(spot - a + half, half)]
-            cross_deep[0] = total
-            for d in range(1, n_th):
-                send(cross_deep.at[0], cross_deep.at[d], along(d), 5)
-
-        return nothing
-
-    lax.fori_loop(0, 2, block, 0)
-
+    landed(cross_plane.at[1:], 9)
+    total = cross_plane[owner]
+    for a in range(1, chunks):
+        total = total + cross_plane[lax.rem(owner - a + chunks, chunks)]
+    cross_deep[0] = total
+    for d in range(1, n_th):
+        send(cross_deep.at[0], cross_deep.at[d], along(d), 10)
+    left(first_pair, 0)
+    left(other_pair, 1)
+    left(first_plane, 2)
+    left(other_plane, 3)
+    beside = tn(corner, first)
+    basis[0:128] = nn(first, mat[0:128]) * scale
+    leaf(work, upper, inverse)
+    landed(cross_deep.at[1:], 10)
+    stores.append(pltpu.make_async_copy(basis.at[0:128], basis_ref.at[0:128], store_sem.at[1]))
+    stores[1].start()
     second = inverse[...]
-    first = inv[0:128, 0:128]
-    corner = upper[...]
-    below = -nn(second, tn(corner, first))
-    inv[128:256, 0:128] = below
-    inv[128:256, 128:256] = second
-
-    landed(cross_deep.at[1:], 5)
+    below = -nn(second, beside)
     cross = cross_deep[th]
     for a in range(1, n_th):
         cross = cross + cross_deep[lax.rem(th - a + n_th, n_th)]
@@ -443,71 +452,56 @@
     padded_low[120:128, 0:128] = low_left
     padded_low[120:128, 128:256] = low_right
     low = jnp.concatenate([low_left, low_right], axis=1)
+    basis[128:256] = (nn(below, mat[0:128]) + nn(second, mat[128:256])) * scale
     snapshot_block = cross_right - nt(low, padded_low[...])
     real = sub8 >= 4
     diagonal = (lane8 == sub8 + 120).astype(jnp.float32)
     snapshot_block = jnp.where(real & (lane8 >= 124), snapshot_block, diagonal)
-    rest_left = -(nn(low_left, first) + nn(low_right, below))
-    rest_right = diagonal - nn(low_right, second)
-    _, _, _, solved = eliminate(
-        spread(snapshot_block, 120), jnp.concatenate([snapshot_block, rest_left, rest_right], axis=1)
-    )
-    real_wide = lax.broadcasted_iota(jnp.int32, (8, 256), 0) >= 4
-    inv[248:256] = jnp.where(real_wide, solved[:, 128:], inv[248:256])
+    rest = snap * scale - nn(low, basis[...])
+    _, _, _, solved = eliminate(spread(snapshot_block, 120), jnp.concatenate([snapshot_block, rest], axis=1))
+    basis[248:256] = jnp.where(place_row >= 4, solved[:, 128:], basis[248:256])
+    stores.append(pltpu.make_async_copy(basis.at[128:256], basis_ref.at[128:256], store_sem.at[2]))
+    stores[2].start()
     turned = padded_low[...].T
-    fac[0:128, 128:256] = jnp.where(column >= 124, turned[0:128], corner) * (1.0 / scale)
-    fac[128:256, 128:256] = jnp.where(column >= 124, turned[128:256], factor_block[...]) * (1.0 / scale)
+    factor[0:128, 128:256] = jnp.where(column >= 124, turned[0:128], corner) * (1.0 / scale)
+    factor[128:256, 128:256] = jnp.where(column >= 124, turned[128:256], upper[...]) * (1.0 / scale)
     finish = jnp.where(lane8 >= sub8 + 120, solved[:, :128] * (1.0 / scale), 0.0)
-    fac[248:256, 128:256] = jnp.where(real, finish, fac[248:256, 128:256])
-
-    stores.append(pltpu.make_async_copy(inv, inverse_ref, store_sem.at[2]))
-    stores.append(pltpu.make_async_copy(fac, factor_ref, store_sem.at[3]))
-    for store in stores[2:]:
-        store.start()
+    factor[248:256, 128:256] = jnp.where(real, finish, factor[248:256, 128:256])
+    stores.append(pltpu.make_async_copy(factor, factor_ref, store_sem.at[3]))
+    stores[3].start()
+
     for stage in range(2):
         for copy in halos[stage]:
             copy.wait_send()
-    left(pair, 0)
-    left(plane, 1)
-    left(deep.at[1:], 2)
-    left(cross_pair.at[0], 3)
-    left(cross_plane.at[1:], 7)
-    left(plane, 4)
-    left(cross_deep.at[1:], 5)
-    left(pair, 6)
+    left(first_deep.at[1:], 4)
+    left(other_deep.at[1:], 5)
+    left(first_plane, 6)
+    left(other_full.at[1:], 7)
+    left(cross_plane.at[1:], 9)
+    left(cross_deep.at[1:], 10)
     for store in stores:
         store.wait()
 
 
-def apply_kernel(
-    scale,
-    new_ref, inverse_ref, factor_ref, matrix_ref,
-    out_new_ref, basis_ref, out_factor_ref,
-    inverse, matrix, new, factor, basis, load_sem, sem,
-):
-    def pieces(source, target, count):
-        rows = source.shape[0] // count
-        return [(source.at[k * rows : (k + 1) * rows], target.at[k * rows : (k + 1) * rows]) for k in range(count)]
-
-    loads = pieces(inverse_ref, inverse, 2) + pieces(matrix_ref, matrix, 2) + [(factor_ref, factor), (new_ref, new)]
-    loads = [pltpu.make_async_copy(source, target, load_sem.at[k]) for k, (source, target) in enumerate(loads)]
+def hand_on_kernel(*refs):
+    count = (len(refs) - 2) // 3
+    sources, targets, held = refs[:count], refs[count : 2 * count], refs[2 * count : 3 * count]
+    load_sem, store_sem = refs[3 * count :]
+    loads, stores = [], []
+    for source, target, through in zip(sources, targets, held):
+        pieces = source.shape[0] // 128 if len(source.shape) == 2 else source.shape[0] // 2
+        rows = source.shape[0] // pieces
+        for k in range(pieces):
+            part, n = pl.ds(k * rows, rows), len(loads)
+            loads.append(pltpu.make_async_copy(source.at[part], through.at[part], load_sem.at[n]))
+            stores.append(pltpu.make_async_copy(through.at[part], target.at[part], store_sem.at[n]))
     for load in loads:
         load.start()
-    copies = []
-    for h in range(2):
-        rows = slice(128 * h, 128 * h + 128)
-        loads[h].wait()
-        loads[2 + h].wait()
-        basis[rows] = nn(inverse[rows, : 128 * h + 128], matrix[: 128 * h + 128]) * scale
-        copies.append(pltpu.make_async_copy(basis.at[rows], basis_ref.at[rows], sem.at[h]))
-        copies[-1].start()
-        if h == 0:
-            for k, source, target in ((4, factor, out_factor_ref), (5, new, out_new_ref)):
-                loads[k].wait()
-                copies.append(pltpu.make_async_copy(source, target, sem.at[k - 2]))
-                copies[-1].start()
-    for copy in copies:
-        copy.wait()
+    for load, store in zip(loads, stores):
+        load.wait()
+        store.start()
+    for store in stores:
+        store.wait()
 
 
 def on_device(sizes, fields, lapse_field, excision, sample_cells, old_basis):
@@ -516,21 +510,20 @@
     columns = old_basis.shape[1]
     f32 = jnp.float32
     half = n_row * n_ph // 2
-    rows = 256 // (2 * half)
+    rows = 128 // half
     cells = sample_cells.reshape(cr, ct)
     vmem = pltpu.VMEM
     scale = math.sqrt(columns * n_row * n_th * n_ph)
-    between = (
+    outputs = (
         jax.ShapeDtypeStruct(fields.shape, f32),
+        jax.ShapeDtypeStruct((256, columns), f32),
         jax.ShapeDtypeStruct((256, 256), f32),
-        jax.ShapeDtypeStruct((256, 256), f32),
-        jax.ShapeDtypeStruct((256, columns), f32),
     )
-    between = pl.pallas_call(
+    results = pl.pallas_call(
         functools.partial(comm_kernel, sizes, scale),
-        out_shape=between,
+        out_shape=outputs,
         in_specs=[HBM] * 5,
-        out_specs=(HBM,) * 4,
+        out_specs=(HBM,) * 3,
         scratch_shapes=[
             vmem(fields.shape, f32),
             vmem(lapse_field.shape, f32),
@@ -553,27 +546,33 @@
             vmem((2, ct, cp), f32),
             vmem((2, ct, cp), f32),
             vmem((2, ct, cp), f32),
-            vmem((2 * half, rows, 256), f32),
-            vmem((2 * half, rows, 256), f32),
-            vmem((half, rows, 256), f32),
-            vmem((half - 1, rows, 256), f32),
-            vmem((n_th, rows, 256), f32),
-            vmem((2, 4, 256), f32),
-            vmem((half, 4, 256), f32),
+            vmem((4, cr, ct, cp), f32),
+            vmem((half, rows, 128), f32),
+            vmem((half, rows, 128), f32),
+            vmem((half, rows, 128), f32),
+            vmem((half - 1, rows, 128), f32),
+            vmem((n_th, rows, 128), f32),
+            vmem((half, rows, 128), f32),
+            vmem((2, half, rows, 128), f32),
+            vmem((half, rows, 128), f32),
+            vmem((half, rows, 128), f32),
+            vmem((half - 1, rows, 128), f32),
+            vmem((n_th, rows, 128), f32),
+            vmem((2 * half, rows, 128), f32),
+            vmem((2 * half, 4, 256), f32),
             vmem((n_th, 4, 256), f32),
-            vmem((256, 256), f32),
-            vmem((256, 256), f32),
             vmem((128, 256), f32),
             vmem((128, 128), f32),
             vmem((128, 128), f32),
-            vmem((128, 128), f32),
             vmem((128, 256), f32),
+            vmem((256, columns), f32),
+            vmem((256, 256), f32),
             pltpu.SemaphoreType.DMA((5,)),
             pltpu.SemaphoreType.DMA((4,)),
             pltpu.SemaphoreType.DMA((2, 6)),
             pltpu.SemaphoreType.DMA((2, 6)),
-            pltpu.SemaphoreType.DMA((8,)),
-            pltpu.SemaphoreType.DMA((8,)),
+            pltpu.SemaphoreType.DMA((11,)),
+            pltpu.SemaphoreType.DMA((11,)),
         ],
         compiler_params=pltpu.CompilerParams(
             collective_id=0, has_side_effects=True, vmem_limit_bytes=LIMIT
@@ -581,26 +580,15 @@
         name="halo_and_gram",
     )(fields, lapse_field, excision, cells, old_basis)
     return pl.pallas_call(
-        functools.partial(apply_kernel, scale),
-        out_shape=(
-            jax.ShapeDtypeStruct(fields.shape, f32),
-            jax.ShapeDtypeStruct((256, columns), f32),
-            jax.ShapeDtypeStruct((256, 256), f32),
-        ),
-        in_specs=[HBM] * 4,
+        hand_on_kernel,
+        out_shape=outputs,
+        in_specs=[HBM] * 3,
         out_specs=(HBM,) * 3,
-        scratch_shapes=[
-            vmem((256, 256), f32),
-            vmem((256, columns), f32),
-            vmem(fields.shape, f32),
-            vmem((256, 256), f32),
-            vmem((256, columns), f32),
-            pltpu.SemaphoreType.DMA((6,)),
-            pltpu.SemaphoreType.DMA((4,)),
-        ],
+        scratch_shapes=[vmem(output.shape, f32) for output in outputs]
+        + [pltpu.SemaphoreType.DMA((7,)), pltpu.SemaphoreType.DMA((7,))],
         compiler_params=pltpu.CompilerParams(vmem_limit_bytes=LIMIT),
-        name="apply",
-    )(*between)
+        name="hand_on",
+    )(*results)
 
 
 def solution(mesh):

time: 46.4 us -> 41.6 us (0.90)
  Pallas kernels: 45.7 us -> 40.7 us
    pallas_call x2, Pallas kernels: 45.7 us -> 40.7 us  [the longest x1 38.4 us: on_device(): pl.pallas_call(functools.partial(comm_kernel, sizes, scale), out_shape=ou...]
where the time goes in v3:
time: 41.6 us; the launch traced here: 41.5 us
  Pallas kernels  40.7 us (98%)
  between operations  0.8 us (2%)
    pallas_call x1, Pallas kernels, on_device(): pl.pallas_call(functools.partial(comm_kernel, sizes, scale), out_shape=ou...  38.4 us
    pallas_call x1, Pallas kernels, on_device(): pl.pallas_call(hand_on_kernel, out_shape=outputs, in_specs=[HBM] * 3, out...  2.31 us

profile of v3, /device:TPU:1, one launch (start us, length us, event | category | flops | bytes accessed | tf_op | source)
XLA Modules:
  0.0 41.5 jit_solution(14705967343783708529)
XLA Ops:
  0.6 38.4 %halo_and_gram.1 = (f32[6,16,16,128]{3,2,1,0:T(8,128)}, f32[256,768]{1,0:T(8,128)}, f32[256,256]{1,0:T(8,128)}) custom-call(f32[6,16,16,128]{3,2,1,0:T(8,128)} %fields_ref.1, f32[16,16,128]{2,1,0:T(8,128)} %lapse_ref.1, s32[16,16,128]{2,1,0:T(8,128)} %excision_ref.1, s32[16,16]{1,0:T(8,128)} %bitcast.1, f32[252,768]{1,0:T(8,128)} %old_ref.1), custom_call_target="tpu_custom_call" | custom-call | tf_op jit(solution)/shard_map/halo_and_gram/pallas_call | solution.py:522
  39.0 2.3 %hand_on.1 = (f32[6,16,16,128]{3,2,1,0:T(8,128)}, f32[256,768]{1,0:T(8,128)}, f32[256,256]{1,0:T(8,128)}) custom-call(f32[6,16,16,128]{3,2,1,0:T(8,128)} %get-tuple-element.6.refs_0_, f32[256,768]{1,0:T(8,128)} %get-tuple-element.7.refs_1_, f32[256,256]{1,0:T(8,128)} %get-tuple-element.8.refs_2_), custom_call_target="tpu_custom_call" | custom-call | tf_op jit(solution)/shard_map/hand_on/pallas_call | solution.py:582

commit v4 on v3

--- a/solution.py
+++ b/solution.py
@@ -11,6 +11,7 @@
 MESH = pl.DeviceIdType.MESH
 LIMIT = 63 * 1024 * 1024
 UNROLL = 2
+MIDWAY = 10
 HIGH = lax.Precision.HIGHEST
 HBM = pl.BlockSpec(memory_space=pltpu.HBM)
 
@@ -72,36 +73,45 @@
     return jnp.concatenate([x, x], axis=1)
 
 
-def leaf(work, upper, inverse):
+def leaf(work, upper, inverse, midway=None):
+    lane = lax.broadcasted_iota(jnp.int32, (8, 128), 1)
+    sub = lax.broadcasted_iota(jnp.int32, (8, 128), 0)
+    tiles = {t: work[8 * t : 8 * t + 8] for t in range(2)}
+    columns = spread(tiles[0], 0)
     for p in range(16):
+        if p == MIDWAY and midway is not None:
+            midway()
         r0 = 8 * p
-        x = work[r0 : r0 + 8]
-        state = {}
-        if p < 15:
-            state["x"] = work[r0 + 8 : r0 + 16]
-            state["e"] = spread(state["x"], r0)
+        if p < 14:
+            tiles[p + 2] = work[r0 + 16 : r0 + 24]
+        near = spread(tiles[p + 1], r0) if p < 15 else None
+        ahead = spread(tiles[p + 1], r0 + 8) if p < 15 else None
+        far = spread(tiles[p + 2], r0) if p < 14 else None
 
         def follower(k, recip, low, line):
-            mine = state["e"][k] * recip
-            state["x"] = state["x"] - twice(mine) * line
-            for b in range(k + 1, 8):
-                state["e"][b] = state["e"][b] - mine * sublane(low, b)
-
-        lows, recips, rows, solved = eliminate(spread(x, r0), x, follower if p < 15 else None)
-        lane = lax.broadcasted_iota(jnp.int32, (8, 128), 1)
-        sub = lax.broadcasted_iota(jnp.int32, (8, 128), 0)
+            for t, column in ((p + 1, near), (p + 2, far)):
+                if column is None:
+                    continue
+                mine = column[k] * recip
+                tiles[t] = tiles[t] - twice(mine) * line
+                for b in range(k + 1, 8):
+                    column[b] = column[b] - mine * sublane(low, b)
+                if t == p + 1:
+                    for b in range(8):
+                        ahead[b] = ahead[b] - mine * sublane(mine, b)
+
+        lows, recips, rows, solved = eliminate(columns, tiles[p], follower)
         upper[r0 : r0 + 8] = jnp.where(lane >= sub + r0, solved[:, :128], 0.0)
         inverse[r0 : r0 + 8] = solved[:, 128:]
-        if p < 15:
-            work[r0 + 8 : r0 + 16] = state["x"]
-        if p < 14:
+        columns = ahead
+        if p < 13:
             back = [None] * 8
             for q in range(7, -1, -1):
                 value = rows[q]
                 for a in range(q + 1, 8):
                     value = value - twice(sublane(lows[q], a)) * back[a]
                 back[q] = value * twice(recips[q])
-            for t in range(p + 2, 16):
+            for t in range(p + 3, 16):
                 tile = work[8 * t : 8 * t + 8]
                 for k, column in enumerate(spread(tile, r0)):
                     tile = tile - twice(column) * back[k]
@@ -136,7 +146,14 @@
     loads = [
         pltpu.make_async_copy(source, target, load_sem.at[k])
         for k, (source, target) in enumerate(
-            ((old_ref, old), (fields_ref, field), (lapse_ref, lapse), (excision_ref, excision), (cells_ref, cells))
+            (
+                (old_ref.at[0:128], old.at[0:128]),
+                (fields_ref, field),
+                (lapse_ref, lapse),
+                (excision_ref, excision),
+                (cells_ref, cells),
+                (old_ref.at[128:252], old.at[128:252]),
+            )
         )
     ]
     for load in loads:
@@ -178,11 +195,8 @@
     lane_pair = lax.shift_right_logical(lane, 1)
 
     loads[0].wait()
-    mat[0:248] = old[0:248]
-    mat[248:252] = old[248:252]
-    mat[252:256] = jnp.zeros((4, mat.shape[1]), jnp.float32)
     tiles = first_part.shape
-    first_part[...] = nt(mat[0:128], mat[0:128]).reshape(tiles)
+    first_part[...] = nt(old[0:128], old[0:128]).reshape(tiles)
     pl.semaphore_wait(barrier, chunks - 1 + n_th - 1)
     other = 1 - core
     send(first_part, first_pair, {"row": y * 2 + other}, 0)
@@ -337,6 +351,9 @@
     first_sum[...] = first_part[...] + first_pair[...]
     for d in range(1, half):
         send(first_sum.at[lax.rem(spot + d, half)], first_plane.at[d - 1], in_half(d), 2)
+    mat[0:248] = old[0:248]
+    mat[248:252] = old[248:252]
+    mat[252:256] = jnp.zeros((4, mat.shape[1]), jnp.float32)
     remaining = nt(mat[128:256], mat[...])
     other_part[0] = remaining[:, :128].reshape(tiles)
     other_part[1] = remaining[:, 128:].reshape(tiles)
@@ -381,6 +398,7 @@
         copy.wait_recv()
     zero_ends(1)
     unrolled(second_step, 0)
+    sample(1)
     landed(first_deep.at[1:], 4)
     total = first_deep[th]
     for a in range(1, n_th):
@@ -388,7 +406,6 @@
     first_full[spot] = total
     for d in range(1, half):
         send(first_full.at[spot], first_full.at[spot], in_half(d), 6)
-    sample(1)
     place_row = lax.broadcasted_iota(jnp.int32, (8, mat.shape[1]), 0)
     snap = jnp.where(place_row >= 4, mat[248:256], 0.0)
     cross_plane[0] = nt(snap, mat[...])[4:8]
@@ -412,7 +429,20 @@
 
     landed(first_plane, 6)
     work[:, :128] = first_full[...].reshape(128, 128)
-    leaf(work, upper, inverse)
+    def sum_cross():
+        landed(cross_plane.at[1:], 9)
+        total = cross_plane[owner]
+        for a in range(1, chunks):
+            total = total + cross_plane[lax.rem(owner - a + chunks, chunks)]
+        cross_deep[0] = total
+        for d in range(1, n_th):
+            send(cross_deep.at[0], cross_deep.at[d], along(d), 10)
+        left(first_pair, 0)
+        left(other_pair, 1)
+        left(first_plane, 2)
+        left(other_plane, 3)
+
+    leaf(work, upper, inverse, sum_cross)
     landed(other_full.at[1:], 7)
     first = inverse[...]
     factor[0:128, 0:128] = upper[...] * (1.0 / scale)
@@ -420,17 +450,6 @@
     last = (square >= 124) | (column >= 124)
     work[:, :128] = jnp.where(last, unit, other_full[half:chunks].reshape(128, 128) - tn(corner, corner))
     work[:, 128:] = unit
-    landed(cross_plane.at[1:], 9)
-    total = cross_plane[owner]
-    for a in range(1, chunks):
-        total = total + cross_plane[lax.rem(owner - a + chunks, chunks)]
-    cross_deep[0] = total
-    for d in range(1, n_th):
-        send(cross_deep.at[0], cross_deep.at[d], along(d), 10)
-    left(first_pair, 0)
-    left(other_pair, 1)
-    left(first_plane, 2)
-    left(other_plane, 3)
     beside = tn(corner, first)
     basis[0:128] = nn(first, mat[0:128]) * scale
     leaf(work, upper, inverse)
@@ -567,7 +586,7 @@
             vmem((128, 256), f32),
             vmem((256, columns), f32),
             vmem((256, 256), f32),
-            pltpu.SemaphoreType.DMA((5,)),
+            pltpu.SemaphoreType.DMA((6,)),
             pltpu.SemaphoreType.DMA((4,)),
             pltpu.SemaphoreType.DMA((2, 6)),
             pltpu.SemaphoreType.DMA((2, 6)),

time: 41.6 us -> 39.7 us (0.954)
  Pallas kernels: 40.7 us -> 38.8 us
    pallas_call x1, Pallas kernels: 38.4 us -> 36.5 us  [on_device(): pl.pallas_call(functools.partial(comm_kernel, sizes, scale), out_shape=ou...]
where the time goes in v4:
time: 39.7 us; the launch traced here: 39.6 us
  Pallas kernels  38.8 us (98%)
  between operations  0.8 us (2%)
    pallas_call x1, Pallas kernels, on_device(): pl.pallas_call(functools.partial(comm_kernel, sizes, scale), out_shape=ou...  36.5 us
    pallas_call x1, Pallas kernels, on_device(): pl.pallas_call(hand_on_kernel, out_shape=outputs, in_specs=[HBM] * 3, out...  2.31 us

profile of v4, /device:TPU:1, one launch (start us, length us, event | category | flops | bytes accessed | tf_op | source)
XLA Modules:
  0.0 39.6 jit_solution(3608747580146485457)
XLA Ops:
  0.6 36.5 %halo_and_gram.1 = (f32[6,16,16,128]{3,2,1,0:T(8,128)}, f32[256,768]{1,0:T(8,128)}, f32[256,256]{1,0:T(8,128)}) custom-call(f32[6,16,16,128]{3,2,1,0:T(8,128)} %fields_ref.1, f32[16,16,128]{2,1,0:T(8,128)} %lapse_ref.1, s32[16,16,128]{2,1,0:T(8,128)} %excision_ref.1, s32[16,16]{1,0:T(8,128)} %bitcast.1, f32[252,768]{1,0:T(8,128)} %old_ref.1), custom_call_target="tpu_custom_call" | custom-call | tf_op jit(solution)/shard_map/halo_and_gram/pallas_call | solution.py:541
  37.1 2.3 %hand_on.1 = (f32[6,16,16,128]{3,2,1,0:T(8,128)}, f32[256,768]{1,0:T(8,128)}, f32[256,256]{1,0:T(8,128)}) custom-call(f32[6,16,16,128]{3,2,1,0:T(8,128)} %get-tuple-element.6.refs_0_, f32[256,768]{1,0:T(8,128)} %get-tuple-element.7.refs_1_, f32[256,256]{1,0:T(8,128)} %get-tuple-element.8.refs_2_), custom_call_target="tpu_custom_call" | custom-call | tf_op jit(solution)/shard_map/hand_on/pallas_call | solution.py:601

commit v5 on v4

--- a/solution.py
+++ b/solution.py
@@ -121,13 +121,13 @@
 def comm_kernel(
     sizes, scale,
     fields_ref, lapse_ref, excision_ref, cells_ref, old_ref,
-    new_ref, basis_ref, factor_ref,
+    new_ref, rows_ref, blocks_ref, cross_ref,
     field, lapse, excision, cells, old, mat, fresh, section, weighted, masked0, masked1,
     padded0, padded1, polar_out0, polar_out1, polar_in0, polar_in1, edge_out0, edge_out1, edge_in0, edge_in1, outside,
     first_part, first_pair, first_sum, first_plane, first_deep, first_full,
     other_part, other_pair, other_sum, other_plane, other_deep, other_full,
     cross_plane, cross_deep,
-    work, upper, inverse, padded_low, basis, factor,
+    work, upper, inverse, rows, blocks, cross_sum,
     load_sem, store_sem, halo_send, halo_recv, send_sem, recv_sem,
 ):
     masked, padded = (masked0, masked1), (padded0, padded1)
@@ -383,6 +383,9 @@
     first_deep[0] = total
     for d in range(1, n_th):
         send(first_deep.at[0], first_deep.at[d], along(d), 4)
+    for copy in halos[1][4:]:
+        copy.wait_recv()
+    beyond(1)
     landed(other_plane, 3)
     total = other_sum[spot]
     for d in range(1, half):
@@ -391,9 +394,6 @@
     for d in range(1, n_th):
         send(other_deep.at[0], other_deep.at[d], along(d), 5)
 
-    for copy in halos[1][4:]:
-        copy.wait_recv()
-    beyond(1)
     for copy in halos[1][:4]:
         copy.wait_recv()
     zero_ends(1)
@@ -417,8 +417,6 @@
     column = lax.broadcasted_iota(jnp.int32, (128, 128), 1)
     unit = (square == column).astype(jnp.float32)
     work[:, 128:] = unit
-    factor[128:256, 0:128] = jnp.zeros((128, 128), jnp.float32)
-    padded_low[...] = jnp.zeros_like(padded_low)
     landed(other_deep.at[1:], 5)
     total = other_deep[th]
     for a in range(1, n_th):
@@ -445,49 +443,35 @@
     leaf(work, upper, inverse, sum_cross)
     landed(other_full.at[1:], 7)
     first = inverse[...]
-    factor[0:128, 0:128] = upper[...] * (1.0 / scale)
     corner = nt(first, other_full[0:half].reshape(128, 128))
+    blocks[0] = first
+    blocks[1] = upper[...]
+    blocks[2] = corner
     last = (square >= 124) | (column >= 124)
     work[:, :128] = jnp.where(last, unit, other_full[half:chunks].reshape(128, 128) - tn(corner, corner))
     work[:, 128:] = unit
-    beside = tn(corner, first)
-    basis[0:128] = nn(first, mat[0:128]) * scale
-    leaf(work, upper, inverse)
+    solved_rows = nn(first, mat[0:128])
+    rows[0:128] = solved_rows
+    rows[128:256] = mat[128:256] - tn(corner, solved_rows)
+    blocks[3] = tn(corner, first)
+
+    def hand_over():
+        for source, target in ((rows, rows_ref), (blocks.at[0:4], blocks_ref.at[0:4])):
+            stores.append(pltpu.make_async_copy(source, target, store_sem.at[len(stores)]))
+            stores[-1].start()
+
+    leaf(work, upper, inverse, hand_over)
+    blocks[4] = upper[...]
+    blocks[5] = inverse[...]
+    stores.append(pltpu.make_async_copy(blocks.at[4:6], blocks_ref.at[4:6], store_sem.at[3]))
+    stores[-1].start()
     landed(cross_deep.at[1:], 10)
-    stores.append(pltpu.make_async_copy(basis.at[0:128], basis_ref.at[0:128], store_sem.at[1]))
-    stores[1].start()
-    second = inverse[...]
-    below = -nn(second, beside)
     cross = cross_deep[th]
     for a in range(1, n_th):
         cross = cross + cross_deep[lax.rem(th - a + n_th, n_th)]
-    cross = jnp.concatenate([jnp.zeros((4, 256), jnp.float32), cross], axis=0)
-    cross_left, cross_right = cross[:, :128], cross[:, 128:]
-    lane8 = lax.broadcasted_iota(jnp.int32, (8, 128), 1)
-    sub8 = lax.broadcasted_iota(jnp.int32, (8, 128), 0)
-    inner = jnp.where(lane8 < 124, cross_right, 0.0)
-    low_left = nt(cross_left, first)
-    low_right = jnp.where(lane8 < 124, nt(cross_left, below) + nt(inner, second), 0.0)
-    padded_low[120:128, 0:128] = low_left
-    padded_low[120:128, 128:256] = low_right
-    low = jnp.concatenate([low_left, low_right], axis=1)
-    basis[128:256] = (nn(below, mat[0:128]) + nn(second, mat[128:256])) * scale
-    snapshot_block = cross_right - nt(low, padded_low[...])
-    real = sub8 >= 4
-    diagonal = (lane8 == sub8 + 120).astype(jnp.float32)
-    snapshot_block = jnp.where(real & (lane8 >= 124), snapshot_block, diagonal)
-    rest = snap * scale - nn(low, basis[...])
-    _, _, _, solved = eliminate(spread(snapshot_block, 120), jnp.concatenate([snapshot_block, rest], axis=1))
-    basis[248:256] = jnp.where(place_row >= 4, solved[:, 128:], basis[248:256])
-    stores.append(pltpu.make_async_copy(basis.at[128:256], basis_ref.at[128:256], store_sem.at[2]))
-    stores[2].start()
-    turned = padded_low[...].T
-    factor[0:128, 128:256] = jnp.where(column >= 124, turned[0:128], corner) * (1.0 / scale)
-    factor[128:256, 128:256] = jnp.where(column >= 124, turned[128:256], upper[...]) * (1.0 / scale)
-    finish = jnp.where(lane8 >= sub8 + 120, solved[:, :128] * (1.0 / scale), 0.0)
-    factor[248:256, 128:256] = jnp.where(real, finish, factor[248:256, 128:256])
-    stores.append(pltpu.make_async_copy(factor, factor_ref, store_sem.at[3]))
-    stores[3].start()
+    cross_sum[...] = jnp.concatenate([jnp.zeros((4, 256), jnp.float32), cross], axis=0)
+    stores.append(pltpu.make_async_copy(cross_sum, cross_ref, store_sem.at[4]))
+    stores[-1].start()
 
     for stage in range(2):
         for copy in halos[stage]:
@@ -502,22 +486,70 @@
         store.wait()
 
 
-def hand_on_kernel(*refs):
-    count = (len(refs) - 2) // 3
-    sources, targets, held = refs[:count], refs[count : 2 * count], refs[2 * count : 3 * count]
-    load_sem, store_sem = refs[3 * count :]
-    loads, stores = [], []
-    for source, target, through in zip(sources, targets, held):
-        pieces = source.shape[0] // 128 if len(source.shape) == 2 else source.shape[0] // 2
-        rows = source.shape[0] // pieces
-        for k in range(pieces):
-            part, n = pl.ds(k * rows, rows), len(loads)
-            loads.append(pltpu.make_async_copy(source.at[part], through.at[part], load_sem.at[n]))
-            stores.append(pltpu.make_async_copy(through.at[part], target.at[part], store_sem.at[n]))
+def finish_kernel(
+    scale,
+    new_ref, rows_ref, blocks_ref, cross_ref,
+    out_new_ref, basis_ref, factor_ref,
+    new, rows, blocks, cross_sum, padded_low, basis, factor,
+    load_sem, store_sem,
+):
+    loads = (
+        (blocks_ref, blocks), (cross_ref, cross_sum), (rows_ref.at[128:256], rows.at[128:256]),
+        (rows_ref.at[0:128], rows.at[0:128]), (new_ref, new),
+    )
+    loads = [pltpu.make_async_copy(source, target, load_sem.at[k]) for k, (source, target) in enumerate(loads)]
     for load in loads:
         load.start()
-    for load, store in zip(loads, stores):
+    factor[128:256, 0:128] = jnp.zeros((128, 128), jnp.float32)
+    padded_low[...] = jnp.zeros_like(padded_low)
+    for load in loads[:4]:
         load.wait()
+    first, second, corner = blocks[0], blocks[5], blocks[2]
+    factor[0:128, 0:128] = blocks[1] * (1.0 / scale)
+    basis[0:128] = rows[0:128] * scale
+    below = -nn(second, blocks[3])
+    cross = cross_sum[...]
+    cross_left, cross_right = cross[:, :128], cross[:, 128:]
+    lane8 = lax.broadcasted_iota(jnp.int32, (8, 128), 1)
+    sub8 = lax.broadcasted_iota(jnp.int32, (8, 128), 0)
+    inner = jnp.where(lane8 < 124, cross_right, 0.0)
+    low_left = nt(cross_left, first)
+    low_right = jnp.where(lane8 < 124, nt(cross_left, below) + nt(inner, second), 0.0)
+    padded_low[120:128, 0:128] = low_left
+    padded_low[120:128, 128:256] = low_right
+    low = jnp.concatenate([low_left, low_right], axis=1)
+    place_row = lax.broadcasted_iota(jnp.int32, (8, basis.shape[1]), 0)
+    snap = jnp.where(place_row >= 4, rows[248:256], 0.0)
+    basis[128:256] = nn(second, rows[128:256]) * scale
+    stores = [
+        pltpu.make_async_copy(source, target, store_sem.at[k])
+        for k, (source, target) in enumerate(
+            (
+                (new, out_new_ref),
+                (basis.at[0:128], basis_ref.at[0:128]),
+                (basis.at[128:256], basis_ref.at[128:256]),
+                (factor, factor_ref),
+            )
+        )
+    ]
+    loads[4].wait()
+    for store in stores[:2]:
+        store.start()
+    snapshot_block = cross_right - nt(low, padded_low[...])
+    real = sub8 >= 4
+    diagonal = (lane8 == sub8 + 120).astype(jnp.float32)
+    snapshot_block = jnp.where(real & (lane8 >= 124), snapshot_block, diagonal)
+    rest = snap * scale - nn(low, basis[...])
+    _, _, _, solved = eliminate(spread(snapshot_block, 120), jnp.concatenate([snapshot_block, rest], axis=1))
+    basis[248:256] = jnp.where(place_row >= 4, solved[:, 128:], basis[248:256])
+    turned = padded_low[...].T
+    square = lax.broadcasted_iota(jnp.int32, (128, 128), 0)
+    column = lax.broadcasted_iota(jnp.int32, (128, 128), 1)
+    factor[0:128, 128:256] = jnp.where(column >= 124, turned[0:128], corner) * (1.0 / scale)
+    factor[128:256, 128:256] = jnp.where(column >= 124, turned[128:256], blocks[4]) * (1.0 / scale)
+    finish = jnp.where(lane8 >= sub8 + 120, solved[:, :128] * (1.0 / scale), 0.0)
+    factor[248:256, 128:256] = jnp.where(real, finish, factor[248:256, 128:256])
+    for store in stores[2:]:
         store.start()
     for store in stores:
         store.wait()
@@ -533,6 +565,12 @@
     cells = sample_cells.reshape(cr, ct)
     vmem = pltpu.VMEM
     scale = math.sqrt(columns * n_row * n_th * n_ph)
+    between = (
+        jax.ShapeDtypeStruct(fields.shape, f32),
+        jax.ShapeDtypeStruct((256, columns), f32),
+        jax.ShapeDtypeStruct((6, 128, 128), f32),
+        jax.ShapeDtypeStruct((8, 256), f32),
+    )
     outputs = (
         jax.ShapeDtypeStruct(fields.shape, f32),
         jax.ShapeDtypeStruct((256, columns), f32),
@@ -540,9 +578,9 @@
     )
     results = pl.pallas_call(
         functools.partial(comm_kernel, sizes, scale),
-        out_shape=outputs,
+        out_shape=between,
         in_specs=[HBM] * 5,
-        out_specs=(HBM,) * 3,
+        out_specs=(HBM,) * 4,
         scratch_shapes=[
             vmem(fields.shape, f32),
             vmem(lapse_field.shape, f32),
@@ -583,11 +621,11 @@
             vmem((128, 256), f32),
             vmem((128, 128), f32),
             vmem((128, 128), f32),
-            vmem((128, 256), f32),
             vmem((256, columns), f32),
-            vmem((256, 256), f32),
+            vmem((6, 128, 128), f32),
+            vmem((8, 256), f32),
             pltpu.SemaphoreType.DMA((6,)),
-            pltpu.SemaphoreType.DMA((4,)),
+            pltpu.SemaphoreType.DMA((5,)),
             pltpu.SemaphoreType.DMA((2, 6)),
             pltpu.SemaphoreType.DMA((2, 6)),
             pltpu.SemaphoreType.DMA((11,)),
@@ -599,14 +637,15 @@
         name="halo_and_gram",
     )(fields, lapse_field, excision, cells, old_basis)
     return pl.pallas_call(
-        hand_on_kernel,
+        functools.partial(finish_kernel, scale),
         out_shape=outputs,
-        in_specs=[HBM] * 3,
+        in_specs=[HBM] * 4,
         out_specs=(HBM,) * 3,
-        scratch_shapes=[vmem(output.shape, f32) for output in outputs]
-        + [pltpu.SemaphoreType.DMA((7,)), pltpu.SemaphoreType.DMA((7,))],
+        scratch_shapes=[vmem(array.shape, f32) for array in between]
+        + [vmem((128, 256), f32), vmem((256, columns), f32), vmem((256, 256), f32)]
+        + [pltpu.SemaphoreType.DMA((5,)), pltpu.SemaphoreType.DMA((4,))],
         compiler_params=pltpu.CompilerParams(vmem_limit_bytes=LIMIT),
-        name="hand_on",
+        name="finish",
     )(*results)
 
 

time: 39.7 us -> 39.4 us (level)
  no operation moved by 1% of the time
where the time goes in v5:
time: 39.4 us; the launch traced here: 39.3 us
  Pallas kernels  38.5 us (98%)
  between operations  0.8 us (2%)
    pallas_call x1, Pallas kernels, on_device(): pl.pallas_call(functools.partial(comm_kernel, sizes, scale), out_shape=be...  34.9 us
    pallas_call x1, Pallas kernels, on_device(): pl.pallas_call(functools.partial(finish_kernel, scale), out_shape=outputs...  3.58 us

profile of v5, /device:TPU:1, one launch (start us, length us, event | category | flops | bytes accessed | tf_op | source)
XLA Modules:
  0.0 39.3 jit_solution(6552271804652027527)
XLA Ops:
  0.6 34.9 %halo_and_gram.1 = (f32[6,16,16,128]{3,2,1,0:T(8,128)}, f32[256,768]{1,0:T(8,128)}, f32[6,128,128]{2,1,0:T(8,128)}, f32[8,256]{1,0:T(8,128)}) custom-call(f32[6,16,16,128]{3,2,1,0:T(8,128)} %fields_ref.1, f32[16,16,128]{2,1,0:T(8,128)} %lapse_ref.1, s32[16,16,128]{2,1,0:T(8,128)} %excision_ref.1, s32[16,16]{1,0:T(8,128)} %bitcast.1, f32[252,768]{1,0:T(8,128)} %old_ref.1), custom_call_target="tpu_custom_call" | custom-call | tf_op jit(solution)/shard_map/halo_and_gram/pallas_call | solution.py:579
  35.5 3.6 %finish.1 = (f32[6,16,16,128]{3,2,1,0:T(8,128)}, f32[256,768]{1,0:T(8,128)}, f32[256,256]{1,0:T(8,128)}) custom-call(f32[6,16,16,128]{3,2,1,0:T(8,128)} %get-tuple-element.7.new_ref, f32[256,768]{1,0:T(8,128)} %get-tuple-element.8.rows_ref, f32[6,128,128]{2,1,0:T(8,128)} %get-tuple-element.9.blocks_ref, f32[8,256]{1,0:T(8,128)} %get-tuple-element.10.cross_ref), custom_call_target="tpu_custom_call" | custom-call | tf_op jit(solution)/shard_map/finish/pallas_call | solution.py:639

commit v6 on v5

--- a/solution.py
+++ b/solution.py
@@ -10,7 +10,7 @@
 
 MESH = pl.DeviceIdType.MESH
 LIMIT = 63 * 1024 * 1024
-UNROLL = 2
+UNROLL = 4
 MIDWAY = 10
 HIGH = lax.Precision.HIGHEST
 HBM = pl.BlockSpec(memory_space=pltpu.HBM)
@@ -383,9 +383,6 @@
     first_deep[0] = total
     for d in range(1, n_th):
         send(first_deep.at[0], first_deep.at[d], along(d), 4)
-    for copy in halos[1][4:]:
-        copy.wait_recv()
-    beyond(1)
     landed(other_plane, 3)
     total = other_sum[spot]
     for d in range(1, half):
@@ -394,6 +391,9 @@
     for d in range(1, n_th):
         send(other_deep.at[0], other_deep.at[d], along(d), 5)
 
+    for copy in halos[1][4:]:
+        copy.wait_recv()
+    beyond(1)
     for copy in halos[1][:4]:
         copy.wait_recv()
     zero_ends(1)

time: 39.4 us -> 38.7 us (0.982)
  Pallas kernels: 38.5 us -> 37.8 us
    pallas_call x1, Pallas kernels: 34.9 us -> 34.2 us  [on_device(): pl.pallas_call(functools.partial(comm_kernel, sizes, scale), out_shape=be...]
where the time goes in v6:
time: 38.7 us; the launch traced here: 38.6 us
  Pallas kernels  37.8 us (98%)
  between operations  0.8 us (2%)
    pallas_call x1, Pallas kernels, on_device(): pl.pallas_call(functools.partial(comm_kernel, sizes, scale), out_shape=be...  34.2 us
    pallas_call x1, Pallas kernels, on_device(): pl.pallas_call(functools.partial(finish_kernel, scale), out_shape=outputs...  3.58 us

profile of v6, /device:TPU:1, one launch (start us, length us, event | category | flops | bytes accessed | tf_op | source)
XLA Modules:
  0.0 38.6 jit_solution(13277390311697596783)
XLA Ops:
  0.6 34.2 %halo_and_gram.1 = (f32[6,16,16,128]{3,2,1,0:T(8,128)}, f32[256,768]{1,0:T(8,128)}, f32[6,128,128]{2,1,0:T(8,128)}, f32[8,256]{1,0:T(8,128)}) custom-call(f32[6,16,16,128]{3,2,1,0:T(8,128)} %fields_ref.1, f32[16,16,128]{2,1,0:T(8,128)} %lapse_ref.1, s32[16,16,128]{2,1,0:T(8,128)} %excision_ref.1, s32[16,16]{1,0:T(8,128)} %bitcast.1, f32[252,768]{1,0:T(8,128)} %old_ref.1), custom_call_target="tpu_custom_call" | custom-call | tf_op jit(solution)/shard_map/halo_and_gram/pallas_call | solution.py:579
  34.9 3.6 %finish.1 = (f32[6,16,16,128]{3,2,1,0:T(8,128)}, f32[256,768]{1,0:T(8,128)}, f32[256,256]{1,0:T(8,128)}) custom-call(f32[6,16,16,128]{3,2,1,0:T(8,128)} %get-tuple-element.7.new_ref, f32[256,768]{1,0:T(8,128)} %get-tuple-element.8.rows_ref, f32[6,128,128]{2,1,0:T(8,128)} %get-tuple-element.9.blocks_ref, f32[8,256]{1,0:T(8,128)} %get-tuple-element.10.cross_ref), custom_call_target="tpu_custom_call" | custom-call | tf_op jit(solution)/shard_map/finish/pallas_call | solution.py:639
